TPU v7x, 256 devices: a whole 4x4x8 slice. The times are simulated.
256 devices in a mesh: sp: 32 (over z, x), rep: 8 (over y, core).
Axes of the slice: x: 4, y: 4, z: 8, core: 2. Of those that a mesh axis runs over, the one named last changes fastest.
Arguments:
- incoming_embeddings: bfloat16 [8, 64, 256, 512], P('rep', 'sp'), may hold values from -16 to 16
- output_sensitivity: bfloat16 [8, 64, 256, 512], P('rep', 'sp'), may hold values from -6 to 6
- mixing_prenormal_multiplier: float32 [512], replicated, may hold values from 0.5 to 1.5
- triple_mapping_matrix: bfloat16 [512, 1536], replicated, may hold values from -1 to 1
- head_sharpness: float32 [8], replicated, may hold values from 0.5 to 300
- output_mapping_matrix: bfloat16 [512, 512], replicated, may hold values from -0.25 to 0.25
- residual_arm_factors: float32 [2, 512], replicated, may hold values from 0.5 to 1.5
- locality_prenormal_multiplier: float32 [512], replicated, may hold values from 0.5 to 1.5
- separable_kernel_pair: float32 [2, 3, 3, 512], replicated, may hold values from -2 to 2
Outputs:
- grad_input: bfloat16 [8, 64, 256, 512], P('rep', 'sp')
- grad_qkv: float32 [512, 1536], P('rep')
- grad_proj: float32 [512, 512], P('rep')
- grad_conv: float32 [2, 3, 3, 512], replicated
- grad_scale: float32 [2, 512], replicated
All inputs are finite; a program needn't handle non-finite values.
Results may differ from a plain program's by a relative error of at most 0.0095.
Values may be sent and summed in bfloat16 or wider, within the bound.
A program may use at most 64 MiB of HBM per device.

v0:
```python
import jax
import jax.numpy as jnp
from jax import lax
from jax.sharding import Mesh
from jax.sharding import PartitionSpec as P

D = 512
HEADS = 8
HEAD_DIM = 64
WIDTH = 256
SP = ("sp_0", "sp_1")
REP = ("rep_0", "rep_1")


EPS = 1e-06


def shifted_2(value, axis, steps):
    count = lax.axis_size(axis)
    leading, last = (max(0, -steps), min(count, count - steps))
    return lax.ppermute(value, axis, [(source, source + steps) for source in range(leading, last)])


def padded_2(block, sides, width):
    for axis, dim in sides:
        count = lax.axis_size(axis)
        forward = [(i, i + 1) for i in range(count - 1)]
        backward = [(target, source) for source, target in forward]
        low = lax.ppermute(
            lax.slice_in_dim(block, block.shape[dim] - width, None, axis=dim), axis, forward
        )
        high = lax.ppermute(lax.slice_in_dim(block, 0, width, axis=dim), axis, backward)
        block = jnp.concatenate([low, block, high], axis=dim)
    return block


def split_up(array, dim, devices):
    before, after = (array.shape[:dim], array.shape[dim + 1 :])
    return jnp.moveaxis(array.reshape(*before, devices, -1, *after), dim, 0)


def sum_at_owner(array, axis, dim):
    tiles = split_up(array, dim, lax.axis_size(axis))
    arrived = lax.all_to_all(tiles, axis, split_axis=0, concat_axis=0, tiled=True)
    return arrived.sum(axis=0)


def rows_for(lines, devices):
    spare = -lines.shape[0] % devices
    if not spare:
        return lines
    return jnp.concatenate([lines, jnp.zeros((spare, *lines.shape[1:]), lines.dtype)])


def in_order(tiles, dim):
    shape = list(tiles.shape[1:])
    shape[dim] *= tiles.shape[0]
    return jnp.moveaxis(tiles, 0, dim).reshape(shape)


def from_everyone(array, axis):
    devices = lax.axis_size(axis)
    return lax.all_to_all(
        jnp.broadcast_to(array[None], (devices, *array.shape)), axis, 0, 0, tiled=True
    )


def gathered_copies(array, axis, dim):
    return in_order(from_everyone(array, axis), dim)


def nested_sum(array, axes):
    own = sum_at_owner(rows_for(array, lax.axis_size(axes)), axes, 0)
    whole = gathered_copies(own, axes, 0)
    return whole[: len(array)].reshape(array.shape)


def packed_total(arrays, axis):
    ends = [0]
    for a in arrays:
        ends.append(ends[-1] + a.size)
    total = nested_sum(jnp.concatenate([a.ravel() for a in arrays]), axis)
    return tuple((total[b:e].reshape(a.shape) for a, b, e in zip(arrays, ends, ends[1:])))


def nested_sum_2(array, axes):
    lines = array.reshape(-1, array.shape[-1])
    padded = rows_for(lines, lax.axis_size(axes))
    whole = gathered_copies(sum_at_owner(padded, axes, 0), axes, 0)
    return lax.slice_in_dim(whole, 0, len(lines)).reshape(array.shape)


def sum_by_axis(array, axes, dim):
    far, near = axes
    own = sum_at_owner(split_up(array, dim, lax.axis_size(far)), near, dim + 1)
    return jnp.sum(lax.all_to_all(own, far, 0, 0, tiled=True), axis=0)


def whole_of(array, axes, dim):
    far, near = axes
    leading = from_everyone(array, far)
    tiles = jnp.swapaxes(from_everyone(leading, near), 0, 1)
    return in_order(tiles.reshape(-1, *array.shape), dim)


def sum_by_parts(array, axes):
    own = sum_by_axis(rows_for(array, lax.axis_size(axes[0]) * lax.axis_size(axes[1])), axes, 0)
    whole = whole_of(own, axes, 0)
    return whole[: len(array)].reshape(array.shape)


def packed_total_2(arrays, axis):
    line, at, outs = (jnp.concatenate([a.reshape(-1) for a in arrays]), 0, [])
    total = sum_by_parts(line, axis)
    for a in arrays:
        outs.append(total[at : at + a.size].reshape(a.shape))
        at += a.size
    return tuple(outs)


def in_one_piece(arrays, axis, dim, along):
    both = jnp.concatenate(arrays, axis=along)
    whole, at, outs = (sum_by_axis(both, axis, dim), 0, [])
    for a in arrays:
        outs.append(lax.slice_in_dim(whole, at, at + a.shape[along], axis=along))
        at += a.shape[along]
    return tuple(outs)


def conv_valid(padded, kernel):
    row_count = padded.shape[0] - 2
    col_count = padded.shape[1] - 2
    total = jnp.zeros((row_count, col_count, padded.shape[2]), jnp.float32)
    for offset_row in range(3):
        for offset_col in range(3):
            total = (
                total
                + padded[offset_row : offset_row + row_count, offset_col : offset_col + col_count]
                * kernel[offset_row, offset_col]
            )
    return total


def gelu_grad(values):
    cumul = 0.5 * (1.0 + lax.erf(values * 0.7071067811865476))
    density = jnp.exp(-0.5 * values * values) * 0.3989422804014327
    return cumul + values * density


def norm_rows(values, gain_vec):
    floated = values.astype(jnp.float32)
    centre = jnp.mean(floated, -1, keepdims=True)
    centred = floated - centre
    variance = jnp.mean(centred * centred, -1, keepdims=True)
    inverse = lax.rsqrt(variance + EPS)
    normed = centred * inverse
    return (normed * gain_vec, normed, inverse)


def norm_back(upstream, gain_vec, normed, inverse):
    scaled = upstream * gain_vec
    return inverse * (
        scaled
        - jnp.mean(scaled, -1, keepdims=True)
        - normed * jnp.mean(scaled * normed, -1, keepdims=True)
    )


def pad_cols(field):
    return jnp.pad(field.astype(jnp.float32), ((0, 0), (1, 1), (0, 0)))


def fold_rims(grad_rows, rim_width):
    top_rim = grad_rows[:rim_width]
    bottom_rim = grad_rows[-rim_width:]
    from_below = shifted_2(top_rim, SP, -1)
    from_above = shifted_2(bottom_rim, SP, 1)
    core_rows = grad_rows[rim_width:-rim_width]
    core_rows = core_rows.at[:rim_width].add(from_above)
    return core_rows.at[-rim_width:].add(from_below)


def local_mix(act_image, separable_kernel_pair, up_two):
    extended = padded_2(act_image, ((SP, 0),), 1)
    padded_in = pad_cols(extended)
    h_one, back_one = jax.vjp(conv_valid, padded_in, separable_kernel_pair[0])
    hidden = jax.nn.gelu(h_one, approximate=False).astype(jnp.bfloat16)
    hidden_ext = padded_2(hidden, ((SP, 0),), 1)
    padded_hid = pad_cols(hidden_ext)
    spatial, back_two = jax.vjp(conv_valid, padded_hid, separable_kernel_pair[1])
    d_pad_hid, grad_w_two = back_two(up_two)
    d_hidden = fold_rims(d_pad_hid[:, 1:-1], 1)
    d_h_one = d_hidden * gelu_grad(h_one)
    d_pad_in, grad_w_one = back_one(d_h_one)
    d_act = fold_rims(d_pad_in[:, 1:-1], 1)
    return (spatial, d_act, jnp.stack([grad_w_one, grad_w_two]))


def shards(
    incoming_embeddings,
    output_sensitivity,
    mixing_prenormal_multiplier,
    triple_mapping_matrix,
    head_sharpness,
    output_mapping_matrix,
    residual_arm_factors,
    locality_prenormal_multiplier,
    separable_kernel_pair,
):
    f32 = jnp.float32
    row_count = incoming_embeddings.shape[1]
    token_count = row_count * WIDTH
    flat_rows = incoming_embeddings.reshape(token_count, D)
    act_one, normed_one, inverse_one = norm_rows(flat_rows, mixing_prenormal_multiplier)
    act_one = act_one.astype(jnp.bfloat16)
    mixed_rows = jnp.dot(act_one, triple_mapping_matrix, preferred_element_type=f32).astype(
        jnp.bfloat16
    )
    query_rows = mixed_rows[:, :D].reshape(token_count, HEADS, HEAD_DIM)
    key_rows = mixed_rows[:, D : 2 * D].reshape(token_count, HEADS, HEAD_DIM)
    value_rows = mixed_rows[:, 2 * D :].reshape(token_count, HEADS, HEAD_DIM)
    query_f = query_rows.astype(f32)
    key_f = key_rows.astype(f32)
    query_sq = jnp.sum(query_f * query_f, 0)
    key_sq = jnp.sum(key_f * key_f, 0)
    gram_part = jnp.einsum("mhc,mhe->hce", query_rows, key_rows, preferred_element_type=f32)
    covariance_accumulated, query_sq, key_sq = packed_total((gram_part, query_sq, key_sq), SP)
    query_norm = jnp.sqrt(query_sq + EPS)
    key_norm = jnp.sqrt(key_sq + EPS)
    softmax_divisor = query_norm[:, :, None] * key_norm[:, None, :]
    feature_affinity_logits = (
        head_sharpness[:, None, None] * covariance_accumulated / softmax_divisor
    )
    shifted = feature_affinity_logits - jnp.max(feature_affinity_logits, -1, keepdims=True)
    exponent = jnp.exp(shifted)
    attn_prob = exponent / jnp.sum(exponent, -1, keepdims=True)
    prob_low = attn_prob.astype(jnp.bfloat16)
    attended = jnp.einsum("hce,mhe->mhc", prob_low, value_rows, preferred_element_type=f32)
    attended = attended.reshape(token_count, D).astype(jnp.bfloat16)
    projected = jnp.dot(attended, output_mapping_matrix, preferred_element_type=f32)
    residual = (flat_rows.astype(f32) + residual_arm_factors[0] * projected).astype(jnp.bfloat16)
    act_two, normed_two, inverse_two = norm_rows(residual, locality_prenormal_multiplier)
    act_two = act_two.astype(jnp.bfloat16)
    upstream = output_sensitivity[0].astype(f32)
    spatial, d_act_image, grad_conv_part = local_mix(
        act_two.reshape(row_count, WIDTH, D),
        separable_kernel_pair,
        residual_arm_factors[1] * upstream,
    )
    up_flat = upstream.reshape(token_count, D)
    scale_two = jnp.sum(spatial.reshape(token_count, D) * up_flat, 0)
    d_residual = up_flat + norm_back(
        d_act_image.reshape(token_count, D), locality_prenormal_multiplier, normed_two, inverse_two
    )
    scale_one = jnp.sum(projected * d_residual, 0)
    d_proj = (residual_arm_factors[0] * d_residual).astype(jnp.bfloat16)
    grad_proj = jnp.einsum("md,me->de", attended, d_proj, preferred_element_type=f32)
    d_attended = lax.dot_general(
        d_proj, output_mapping_matrix, (((1,), (1,)), ((), ())), preferred_element_type=f32
    ).astype(jnp.bfloat16)
    d_att_heads = d_attended.reshape(token_count, HEADS, HEAD_DIM)
    prob_part = jnp.einsum("mhc,mhe->hce", d_att_heads, value_rows, preferred_element_type=f32)
    d_value = jnp.einsum("hce,mhc->mhe", prob_low, d_att_heads, preferred_element_type=f32)
    prob_grad = nested_sum_2(prob_part, SP)
    logit_sensitivity = attn_prob * (prob_grad - jnp.sum(attn_prob * prob_grad, -1, keepdims=True))
    covariance_sensitivity = (
        logit_sensitivity * head_sharpness[:, None, None] / softmax_divisor
    ).astype(jnp.bfloat16)
    weighted = logit_sensitivity * feature_affinity_logits
    d_qsq = -jnp.sum(weighted, -1) / (2.0 * query_norm * query_norm)
    d_ksq = -jnp.sum(weighted, 1) / (2.0 * key_norm * key_norm)
    d_query = (
        jnp.einsum("hce,mhe->mhc", covariance_sensitivity, key_rows, preferred_element_type=f32)
        + 2.0 * d_qsq * query_f
    )
    d_key = (
        jnp.einsum("hce,mhc->mhe", covariance_sensitivity, query_rows, preferred_element_type=f32)
        + 2.0 * d_ksq * key_f
    )
    d_mixed = jnp.concatenate(
        [
            d_query.reshape(token_count, D),
            d_key.reshape(token_count, D),
            d_value.reshape(token_count, D),
        ],
        -1,
    ).astype(jnp.bfloat16)
    grad_qkv = jnp.einsum("md,me->de", act_one, d_mixed, preferred_element_type=f32)
    d_act_one = lax.dot_general(
        d_mixed, triple_mapping_matrix, (((1,), (1,)), ((), ())), preferred_element_type=f32
    )
    d_tokens = (
        d_residual + norm_back(d_act_one, mixing_prenormal_multiplier, normed_one, inverse_one)
    ).astype(jnp.bfloat16)
    grad_conv, grad_scale = packed_total_2(
        (grad_conv_part, jnp.stack([scale_one, scale_two])), (("sp_0", "sp_1"), ("rep_0", "rep_1"))
    )
    partial_rows = in_one_piece((grad_qkv, grad_proj), ("rep_0", "rep_1"), 0, 1)
    grad_qkv, grad_proj = packed_total((partial_rows[0], partial_rows[1]), SP)
    return (d_tokens.reshape(1, row_count, WIDTH, D), grad_qkv, grad_proj, grad_conv, grad_scale)


def solution(mesh):
    torus = Mesh(mesh.devices.reshape(8, 4, 4, 2), ("sp_0", "sp_1", "rep_0", "rep_1"))
    in_specs = (P(REP, SP, None, None), P(REP, SP, None, None), P(), P(), P(), P(), P(), P(), P())
    out_specs = (P(REP, SP, None, None), P(REP, None), P(REP, None), P(), P())
    return jax.shard_map(
        shards, mesh=torus, in_specs=in_specs, out_specs=out_specs, check_vma=False
    )
```

profile of v0, /device:TPU:1, one launch (start us, length us, event | category | flops | bytes accessed | tf_op | source)
XLA Modules:
  0.0 307.1 jit_solution(2386367674989689349)
XLA Ops:
  10.6 11.9 %all-to-all-start = ((f32[32,1,1056]{2,1,0:T(1,128)}), f32[32,1,1056]{2,1,0:T(1,128)S(1)}, u32[]{:S(2)}, u32[]{:S(2)}) async-start(f32[32,1,1056]{2,1,0:T(1,128)} %all_to_all.48), calls=%async_computation | async-start | bytes 294912 | tf_op jit(solution)/shard_map/all_to_all | solution.py:44
  27.9 4.0 %all-to-all-done = f32[32,1,1056]{2,1,0:T(1,128)S(1)} async-done(((f32[32,1,1056]{2,1,0:T(1,128)}), f32[32,1,1056]{2,1,0:T(1,128)S(1)}, u32[]{:S(2)}, u32[]{:S(2)}) %all-to-all-start) | async-done | bytes 135200 | tf_op jit(solution)/shard_map/all_to_all | solution.py:44
  32.7 5.3 %all-to-all-start.1 = ((f32[32,1,1056]{2,1,0:T(1,128)}), f32[32,1,1056]{2,1,0:T(1,128)S(1)}, u32[]{:S(2)}, u32[]{:S(2)}) async-start(f32[32,1,1056]{2,1,0:T(1,128)} %broadcast_in_dim.12), calls=%async_computation.1 | async-start | bytes 294912 | tf_op jit(solution)/shard_map/all_to_all | solution.py:63
  40.4 3.9 %collective-permute-start = (f32[1,256,512]{2,1,0:T(8,128)}, f32[1,256,512]{2,1,0:T(8,128)}, u32[]{:S(2)}, u32[]{:S(2)}) collective-permute-start(f32[1,256,512]{2,1,0:T(8,128)} %get-tuple-element.111), channel_id=1, source_target_pairs={{0,8},{8,16},{16,24},{24,32},{32,40},{40,48},{48,56},{56,64},{64,7... | collective-permute-start | bytes 1572872 | tf_op jit(solution)/shard_map/ppermute | solution.py:21
  58.7 4.0 %collective-permute-start.2 = (bf16[1,256,512]{2,1,0:T(8,128)(2,1)S(1)}, bf16[1,256,512]{2,1,0:T(8,128)(2,1)S(1)}, u32[]{:S(2)}, u32[]{:S(2)}) collective-permute-start(bf16[1,256,512]{2,1,0:T(8,128)(2,1)S(1)} %get-tuple-element.136), channel_id=1, source_target_pairs={{0,8},{8,16},{16,24},{24,32},{32,40},{40,48},{48,56},{56,64},{64,7... | collective-permute-start | bytes 786440 | tf_op jit(solution)/shard_map/ppermute | solution.py:29
  82.5 5.8 %collective-permute-start.4 = (f32[1,256,512]{2,1,0:T(8,128)}, f32[1,256,512]{2,1,0:T(8,128)}, u32[]{:S(2)}, u32[]{:S(2)}) collective-permute-start(f32[1,256,512]{2,1,0:T(8,128)} %get-tuple-element.109), channel_id=1, source_target_pairs={{0,8},{8,16},{16,24},{24,32},{32,40},{40,48},{48,56},{56,64},{64,7... | collective-permute-start | bytes 1572872 | tf_op jit(solution)/shard_map/ppermute | solution.py:21
  93.2 5.5 %fusion.23 = f32[512]{0:T(512)S(1)} fusion(f32[4,256,512]{2,1,0:T(8,128)} %copy-done.1, bf16[1,2,256,512]{3,2,1,0:T(8,128)(2,1)} %param.18, f32[512]{0:T(512)} %bitcast.244, f32[512]{0:T(512)} %bitcast.246, f32[512]{0:T(512)} %bitcast.248, f32[512]{0:T(512)} %bitcast.250, f32[512]{0:T(512)} %bitcast.252, f32[512]{0:T(512)} %bitcast.254, f32[512]{0:T(512)} %bitcast.256, ...), kind=kLoop, calls=%fused_computation.56 | loop fusion | flops 5242368 | bytes 5787648 | tf_op jit(solution)/shard_map/reduce_sum | solution.py:251
  105.5 9.4 %all-to-all-start.8 = ((f32[8,1,1280]{2,1,0:T(1,128)}), f32[8,1,1280]{2,1,0:T(1,128)}, u32[]{:S(2)}, u32[]{:S(2)}) async-start(f32[8,1,1280]{2,1,0:T(1,128)} %reshape.493), calls=%async_computation.8 | async-start | bytes 81920 | tf_op jit(solution)/shard_map/all_to_all | solution.py:44
  120.8 16.8 %all-to-all-start.2 = ((f32[32,1,1024]{2,1,0:T(1,128)}), f32[32,1,1024]{2,1,0:T(1,128)}, u32[]{:S(2)}, u32[]{:S(2)}) async-start(f32[32,1,1024]{2,1,0:T(1,128)} %reshape.489), calls=%async_computation.2 | async-start | bytes 262144 | tf_op jit(solution)/shard_map/all_to_all | solution.py:44
  149.4 9.3 %all-to-all-start.9 = ((f32[32,1,40]{2,1,0:T(1,128)}), f32[32,1,40]{2,1,0:T(1,128)}, u32[]{:S(2)}, u32[]{:S(2)}) async-start(f32[32,1,40]{2,1,0:T(1,128)} %bitcast.70), calls=%async_computation.9 | async-start | bytes 32768 | tf_op jit(solution)/shard_map/all_to_all | solution.py:96
  164.1 3.0 all-to-all-done.9
  167.1 6.2 %all-to-all-start.3 = ((f32[32,1,1024]{2,1,0:T(1,128)}), f32[32,1,1024]{2,1,0:T(1,128)}, u32[]{:S(2)}, u32[]{:S(2)}) async-start(f32[32,1,1024]{2,1,0:T(1,128)} %reshape.491), calls=%async_computation.3 | async-start | bytes 262144 | tf_op jit(solution)/shard_map/all_to_all | solution.py:63
  177.2 5.4 %all-to-all-done.3 = f32[32,1,1024]{2,1,0:T(1,128)} async-done(((f32[32,1,1024]{2,1,0:T(1,128)}), f32[32,1,1024]{2,1,0:T(1,128)}, u32[]{:S(2)}, u32[]{:S(2)}) %all-to-all-start.3) | async-done | bytes 131104 | tf_op jit(solution)/shard_map/all_to_all | solution.py:63
  193.6 10.4 %all_to_all.75 = f32[2,4,64,2048]{3,2,1,0:T(8,128)} all-to-all(f32[2,4,64,2048]{3,2,1,0:T(8,128)S(1)} %bitcast.211), channel_id=1, replica_groups=mesh['sp_0'=8,'sp_1'=4,'rep_0'=4,'rep_1'=2] {'rep_1'}, dimensions={0} | all-to-all | bytes 8388608 | tf_op jit(solution)/shard_map/all_to_all | solution.py:44
  204.6 3.8 %all-to-all-start.10 = ((f32[32,1,40]{2,1,0:T(1,128)}), f32[32,1,40]{2,1,0:T(1,128)S(1)}, u32[]{:S(2)}, u32[]{:S(2)}) async-start(f32[32,1,40]{2,1,0:T(1,128)} %broadcast_in_dim.15), calls=%async_computation.10 | async-start | bytes 32768 | tf_op jit(solution)/shard_map/all_to_all | solution.py:63
  208.4 4.1 %reduce_sum.386 = f32[4,64,2048]{2,1,0:T(8,128)} reduce(f32[2,4,64,2048]{3,2,1,0:T(8,128)} %all_to_all.75, f32[]{:T(128)} %constant.141.clone.1), dimensions={0}, to_apply=%region_17.18 | reduce | flops 524288 | bytes 6291460 | tf_op jit(solution)/shard_map/reduce_sum | solution.py:45
  212.5 4.5 %all-to-all-done.10 = f32[32,1,40]{2,1,0:T(1,128)S(1)} async-done(((f32[32,1,40]{2,1,0:T(1,128)}), f32[32,1,40]{2,1,0:T(1,128)S(1)}, u32[]{:S(2)}, u32[]{:S(2)}) %all-to-all-start.10) | async-done | bytes 5152 | tf_op jit(solution)/shard_map/all_to_all | solution.py:63
  217.0 4.6 %all-to-all-start.5 = ((f32[4,64,2048]{2,1,0:T(8,128)}), f32[4,64,2048]{2,1,0:T(8,128)}, u32[]{:S(2)}, u32[]{:S(2)}) async-start(f32[4,64,2048]{2,1,0:T(8,128)} %reduce_sum.386), calls=%async_computation.5 | async-start | bytes 4194304 | tf_op jit(solution)/shard_map/all_to_all | solution.py:96
  222.4 24.4 %all-to-all-done.5 = f32[4,64,2048]{2,1,0:T(8,128)} async-done(((f32[4,64,2048]{2,1,0:T(8,128)}), f32[4,64,2048]{2,1,0:T(8,128)}, u32[]{:S(2)}, u32[]{:S(2)}) %all-to-all-start.5) | async-done | bytes 2097184 | tf_op jit(solution)/shard_map/all_to_all | solution.py:96
  246.7 6.3 %all-to-all-start.11 = ((f32[8,1,1280]{2,1,0:T(1,128)}), f32[8,1,1280]{2,1,0:T(1,128)}, u32[]{:S(2)}, u32[]{:S(2)}) async-start(f32[8,1,1280]{2,1,0:T(1,128)} %reshape.495), calls=%async_computation.11 | async-start | bytes 81920 | tf_op jit(solution)/shard_map/all_to_all | solution.py:63
  257.9 4.8 %all-to-all-start.6 = ((f32[32,1,4096]{2,1,0:T(1,128)}), f32[32,1,4096]{2,1,0:T(1,128)}, u32[]{:S(2)}, u32[]{:S(2)}) async-start(f32[32,1,4096]{2,1,0:T(1,128)} %bitcast.224), calls=%async_computation.6 | async-start | bytes 1048576 | tf_op jit(solution)/shard_map/all_to_all | solution.py:44
  266.0 12.9 %all-to-all-done.6 = f32[32,1,4096]{2,1,0:T(1,128)} async-done(((f32[32,1,4096]{2,1,0:T(1,128)}), f32[32,1,4096]{2,1,0:T(1,128)}, u32[]{:S(2)}, u32[]{:S(2)}) %all-to-all-start.6) | async-done | bytes 524320 | tf_op jit(solution)/shard_map/all_to_all | solution.py:44
  281.6 5.7 %all-to-all-start.7 = ((f32[32,1,4096]{2,1,0:T(1,128)}), f32[32,1,4096]{2,1,0:T(1,128)}, u32[]{:S(2)}, u32[]{:S(2)}) async-start(f32[32,1,4096]{2,1,0:T(1,128)} %broadcast_in_dim.14), calls=%async_computation.7 | async-start | bytes 1048576 | tf_op jit(solution)/shard_map/all_to_all | solution.py:63
  291.2 11.0 %all-to-all-done.7 = f32[32,1,4096]{2,1,0:T(1,128)} async-done(((f32[32,1,4096]{2,1,0:T(1,128)}), f32[32,1,4096]{2,1,0:T(1,128)}, u32[]{:S(2)}, u32[]{:S(2)}) %all-to-all-start.7) | async-done | bytes 524320 | tf_op jit(solution)/shard_map/all_to_all | solution.py:63
  (285 shorter events, 121.8 us)
Async XLA Ops:
  10.6 21.3 %all-to-all-start = ((f32[32,1,1056]{2,1,0:T(1,128)}), f32[32,1,1056]{2,1,0:T(1,128)S(1)}, u32[]{:S(2)}, u32[]{:S(2)}) async-start(f32[32,1,1056]{2,1,0:T(1,128)} %all_to_all.48), calls=%async_computation | async-start | bytes 294912 | tf_op jit(solution)/shard_map/all_to_all | solution.py:44
  32.7 16.2 %all-to-all-start.1 = ((f32[32,1,1056]{2,1,0:T(1,128)}), f32[32,1,1056]{2,1,0:T(1,128)S(1)}, u32[]{:S(2)}, u32[]{:S(2)}) async-start(f32[32,1,1056]{2,1,0:T(1,128)} %broadcast_in_dim.12), calls=%async_computation.1 | async-start | bytes 294912 | tf_op jit(solution)/shard_map/all_to_all | solution.py:63
  40.4 23.7 %collective-permute-start = (f32[1,256,512]{2,1,0:T(8,128)}, f32[1,256,512]{2,1,0:T(8,128)}, u32[]{:S(2)}, u32[]{:S(2)}) collective-permute-start(f32[1,256,512]{2,1,0:T(8,128)} %get-tuple-element.111), channel_id=1, source_target_pairs={{0,8},{8,16},{16,24},{24,32},{32,40},{40,48},{48,56},{56,64},{64,7... | collective-permute-start | bytes 1572872 | tf_op jit(solution)/shard_map/ppermute | solution.py:21
  44.3 21.2 %collective-permute-start.1 = (f32[1,256,512]{2,1,0:T(8,128)}, f32[1,256,512]{2,1,0:T(8,128)}, u32[]{:S(2)}, u32[]{:S(2)}) collective-permute-start(f32[1,256,512]{2,1,0:T(8,128)} %get-tuple-element.110), channel_id=1, source_target_pairs={{8,0},{16,8},{24,16},{32,24},{40,32},{48,40},{56,48},{64,56},{72,6... | collective-permute-start | bytes 1572872 | tf_op jit(solution)/shard_map/ppermute | solution.py:21
  58.7 8.1 %collective-permute-start.2 = (bf16[1,256,512]{2,1,0:T(8,128)(2,1)S(1)}, bf16[1,256,512]{2,1,0:T(8,128)(2,1)S(1)}, u32[]{:S(2)}, u32[]{:S(2)}) collective-permute-start(bf16[1,256,512]{2,1,0:T(8,128)(2,1)S(1)} %get-tuple-element.136), channel_id=1, source_target_pairs={{0,8},{8,16},{16,24},{24,32},{32,40},{40,48},{48,56},{56,64},{64,7... | collective-permute-start | bytes 786440 | tf_op jit(solution)/shard_map/ppermute | solution.py:29
  62.7 7.1 %collective-permute-start.3 = (bf16[1,256,512]{2,1,0:T(8,128)(2,1)S(1)}, bf16[1,256,512]{2,1,0:T(8,128)(2,1)S(1)}, u32[]{:S(2)}, u32[]{:S(2)}) collective-permute-start(bf16[1,256,512]{2,1,0:T(8,128)(2,1)S(1)} %get-tuple-element.137), channel_id=1, source_target_pairs={{8,0},{16,8},{24,16},{32,24},{40,32},{48,40},{56,48},{64,56},{72,6... | collective-permute-start | bytes 786440 | tf_op jit(solution)/shard_map/ppermute | solution.py:32
  74.8 14.8 %collective-permute-start.6 = (bf16[1,256,512]{2,1,0:T(8,128)(2,1)S(1)}, bf16[1,256,512]{2,1,0:T(8,128)(2,1)S(1)}, u32[]{:S(2)}, u32[]{:S(2)}) collective-permute-start(bf16[1,256,512]{2,1,0:T(8,128)(2,1)S(1)} %get-tuple-element.134), channel_id=1, source_target_pairs={{0,8},{8,16},{16,24},{24,32},{32,40},{40,48},{48,56},{56,64},{64,7... | collective-permute-start | bytes 786440 | tf_op jit(solution)/shard_map/ppermute | solution.py:29
  77.4 12.2 %collective-permute-start.7 = (bf16[1,256,512]{2,1,0:T(8,128)(2,1)S(1)}, bf16[1,256,512]{2,1,0:T(8,128)(2,1)S(1)}, u32[]{:S(2)}, u32[]{:S(2)}) collective-permute-start(bf16[1,256,512]{2,1,0:T(8,128)(2,1)S(1)} %get-tuple-element.135), channel_id=1, source_target_pairs={{8,0},{16,8},{24,16},{32,24},{40,32},{48,40},{56,48},{64,56},{72,6... | collective-permute-start | bytes 786440 | tf_op jit(solution)/shard_map/ppermute | solution.py:32
  82.5 16.3 %collective-permute-start.4 = (f32[1,256,512]{2,1,0:T(8,128)}, f32[1,256,512]{2,1,0:T(8,128)}, u32[]{:S(2)}, u32[]{:S(2)}) collective-permute-start(f32[1,256,512]{2,1,0:T(8,128)} %get-tuple-element.109), channel_id=1, source_target_pairs={{0,8},{8,16},{16,24},{24,32},{32,40},{40,48},{48,56},{56,64},{64,7... | collective-permute-start | bytes 1572872 | tf_op jit(solution)/shard_map/ppermute | solution.py:21
  88.3 12.9 %collective-permute-start.5 = (f32[1,256,512]{2,1,0:T(8,128)}, f32[1,256,512]{2,1,0:T(8,128)}, u32[]{:S(2)}, u32[]{:S(2)}) collective-permute-start(f32[1,256,512]{2,1,0:T(8,128)} %get-tuple-element.108), channel_id=1, source_target_pairs={{8,0},{16,8},{24,16},{32,24},{40,32},{48,40},{56,48},{64,56},{72,6... | collective-permute-start | bytes 1572872 | tf_op jit(solution)/shard_map/ppermute | solution.py:21
  105.5 15.4 %all-to-all-start.8 = ((f32[8,1,1280]{2,1,0:T(1,128)}), f32[8,1,1280]{2,1,0:T(1,128)}, u32[]{:S(2)}, u32[]{:S(2)}) async-start(f32[8,1,1280]{2,1,0:T(1,128)} %reshape.493), calls=%async_computation.8 | async-start | bytes 81920 | tf_op jit(solution)/shard_map/all_to_all | solution.py:44
  114.9 43.8 %copy-start.2 = (f32[512,512]{1,0:T(8,128)S(1)}, f32[512,512]{1,0:T(8,128)}, u32[]{:S(2)}) copy-start(f32[512,512]{1,0:T(8,128)} %get-tuple-element.105) | copy-start | bytes 3145732
  116.8 44.4 %copy-start.16 = (bf16[512,512]{0,1:T(8,128)(2,1)}, bf16[512,512]{0,1:T(8,128)(2,1)S(1)}, u32[]{:S(2)}) copy-start(bf16[512,512]{0,1:T(8,128)(2,1)S(1)} %convolution_convert_fusion.3) | copy-start | bytes 1572868
  120.8 28.6 %all-to-all-start.2 = ((f32[32,1,1024]{2,1,0:T(1,128)}), f32[32,1,1024]{2,1,0:T(1,128)}, u32[]{:S(2)}, u32[]{:S(2)}) async-start(f32[32,1,1024]{2,1,0:T(1,128)} %reshape.489), calls=%async_computation.2 | async-start | bytes 262144 | tf_op jit(solution)/shard_map/all_to_all | solution.py:44
  149.4 17.7 %all-to-all-start.9 = ((f32[32,1,40]{2,1,0:T(1,128)}), f32[32,1,40]{2,1,0:T(1,128)}, u32[]{:S(2)}, u32[]{:S(2)}) async-start(f32[32,1,40]{2,1,0:T(1,128)} %bitcast.70), calls=%async_computation.9 | async-start | bytes 32768 | tf_op jit(solution)/shard_map/all_to_all | solution.py:96
  167.1 15.6 %all-to-all-start.3 = ((f32[32,1,1024]{2,1,0:T(1,128)}), f32[32,1,1024]{2,1,0:T(1,128)}, u32[]{:S(2)}, u32[]{:S(2)}) async-start(f32[32,1,1024]{2,1,0:T(1,128)} %reshape.491), calls=%async_computation.3 | async-start | bytes 262144 | tf_op jit(solution)/shard_map/all_to_all | solution.py:63
  204.6 12.4 %all-to-all-start.10 = ((f32[32,1,40]{2,1,0:T(1,128)}), f32[32,1,40]{2,1,0:T(1,128)S(1)}, u32[]{:S(2)}, u32[]{:S(2)}) async-start(f32[32,1,40]{2,1,0:T(1,128)} %broadcast_in_dim.15), calls=%async_computation.10 | async-start | bytes 32768 | tf_op jit(solution)/shard_map/all_to_all | solution.py:63
  217.0 29.8 %all-to-all-start.5 = ((f32[4,64,2048]{2,1,0:T(8,128)}), f32[4,64,2048]{2,1,0:T(8,128)}, u32[]{:S(2)}, u32[]{:S(2)}) async-start(f32[4,64,2048]{2,1,0:T(8,128)} %reduce_sum.386), calls=%async_computation.5 | async-start | bytes 4194304 | tf_op jit(solution)/shard_map/all_to_all | solution.py:96
  246.7 11.2 %all-to-all-start.11 = ((f32[8,1,1280]{2,1,0:T(1,128)}), f32[8,1,1280]{2,1,0:T(1,128)}, u32[]{:S(2)}, u32[]{:S(2)}) async-start(f32[8,1,1280]{2,1,0:T(1,128)} %reshape.495), calls=%async_computation.11 | async-start | bytes 81920 | tf_op jit(solution)/shard_map/all_to_all | solution.py:63
  257.3 30.0 %copy-start.51 = (f32[1,2,2,128]{3,1,2,0:T(2,128)S(1)}, f32[1,2,2,128]{3,1,2,0:T(2,128)}, u32[]{:S(2)}) copy-start(f32[1,2,2,128]{3,1,2,0:T(2,128)} %copy-done.50) | copy-start | bytes 6148
  257.3 30.0 %copy-start.53 = (f32[1,2,2,128]{3,1,2,0:T(2,128)S(1)}, f32[1,2,2,128]{3,1,2,0:T(2,128)}, u32[]{:S(2)}) copy-start(f32[1,2,2,128]{3,1,2,0:T(2,128)} %copy-done.52) | copy-start | bytes 6148
  257.3 30.0 %copy-start.64 = (f32[512]{0:T(512)S(1)}, f32[512]{0:T(512)}, u32[]{:S(2)}) copy-start(f32[512]{0:T(512)} %param.19) | copy-start | bytes 6148
  257.9 21.0 %all-to-all-start.6 = ((f32[32,1,4096]{2,1,0:T(1,128)}), f32[32,1,4096]{2,1,0:T(1,128)}, u32[]{:S(2)}, u32[]{:S(2)}) async-start(f32[32,1,4096]{2,1,0:T(1,128)} %bitcast.224), calls=%async_computation.6 | async-start | bytes 1048576 | tf_op jit(solution)/shard_map/all_to_all | solution.py:44
  281.6 20.7 %all-to-all-start.7 = ((f32[32,1,4096]{2,1,0:T(1,128)}), f32[32,1,4096]{2,1,0:T(1,128)}, u32[]{:S(2)}, u32[]{:S(2)}) async-start(f32[32,1,4096]{2,1,0:T(1,128)} %broadcast_in_dim.14), calls=%async_computation.7 | async-start | bytes 1048576 | tf_op jit(solution)/shard_map/all_to_all | solution.py:63
  (62 other events, 370.5 us)
where the time goes:
time: 311 us; the launch traced here: 307 us
  starting transfers between devices  106 us (34%)
  waiting for transfers between devices  69.9 us (22%)
  other arithmetic  56.6 us (18%)
  local copies, waits for them, and re-layouts  43.8 us (14%)
  matrix products  18.4 us (6%)
  blocking collectives  10.4 us (3%)
    all_to_all x4, starting transfers between devices, sum_at_owner(): lax.all_to_all(tiles, axis, split_axis=0, concat_axis=0, tiled=True)  42.9 us
    all_to_all x2, waiting for transfers between devices, sum_by_axis(): return jnp.sum(lax.all_to_all(own, far, 0, 0, tiled=True), axis=0)  27.4 us
    all_to_all x5, starting transfers between devices, from_everyone(): lax.all_to_all(jnp.broadcast_to(array[None], (devices, *array.shape)), ax...  27.3 us
    all_to_all x5, waiting for transfers between devices, from_everyone(): lax.all_to_all(jnp.broadcast_to(array[None], (devices, *array.shape)), ax...  21.6 us
    all_to_all x4, waiting for transfers between devices, sum_at_owner(): lax.all_to_all(tiles, axis, split_axis=0, concat_axis=0, tiled=True)  16.9 us
    all_to_all x2, starting transfers between devices, sum_by_axis(): return jnp.sum(lax.all_to_all(own, far, 0, 0, tiled=True), axis=0)  13.9 us
    ppermute x4, starting transfers between devices, shifted_2(): lax.ppermute(value, axis, [(source, source + steps) for source in range(l...  12.3 us
    unnamed x150, local copies, waits for them, and re-layouts  10.5 us
  transfers between devices with their start and end apart: 19, of which 10 were waited for; matrix products, arithmetic and copies ran while one was open for 26% of the time, Pallas kernels for 0%

commit v1 on v0

v1 whole, which is shorter than its diff:
```python
import functools

import jax
import jax.numpy as jnp
from jax import lax
from jax.experimental import pallas as pl
from jax.experimental.pallas import tpu as pltpu
from jax.sharding import PartitionSpec as P

D = 512
HEADS = 8
HEAD_DIM = 64
WIDTH = 256
EPS = 1e-06
F32 = jnp.float32
BF16 = jnp.bfloat16
TOK = 512
PAIRS = 4
VMEM = pltpu.VMEM
MESH_ID = pl.DeviceIdType.MESH
LIMIT = 60 * 1024 * 1024


def dot(a, b, ca, cb):
    return lax.dot_general(a, b, (((ca,), (cb,)), ((), ())), preferred_element_type=F32)


def ds(start, size, multiple=None):
    return pl.ds(pl.multiple_of(start, multiple or size), size)


def norm_parts(u):
    centre = jnp.mean(u, -1, keepdims=True)
    centred = u - centre
    inverse = lax.rsqrt(jnp.mean(centred * centred, -1, keepdims=True) + EPS)
    return centred * inverse, inverse


def norm_back(upstream, gain, normed, inverse):
    scaled = upstream * gain
    return inverse * (
        scaled
        - jnp.mean(scaled, -1, keepdims=True)
        - normed * jnp.mean(scaled * normed, -1, keepdims=True)
    )


def lane_low():
    return lax.broadcasted_iota(jnp.int32, (HEAD_DIM, 128), 1) < HEAD_DIM


def eye_pair():
    lane = lax.broadcasted_iota(jnp.int32, (HEAD_DIM, 128), 1)
    row = lax.broadcasted_iota(jnp.int32, (HEAD_DIM, 128), 0)
    return (lane == row) | (lane == row + HEAD_DIM)


def half_sum(v, low):
    left = jnp.sum(jnp.where(low, v, 0.0), -1, keepdims=True)
    right = jnp.sum(jnp.where(low, 0.0, v), -1, keepdims=True)
    return jnp.where(low, left, right)


def half_max(v, low):
    left = jnp.max(jnp.where(low, v, -jnp.inf), -1, keepdims=True)
    right = jnp.max(jnp.where(low, -jnp.inf, v), -1, keepdims=True)
    return jnp.where(low, left, right)


def pack_pair(full, low):
    return jnp.where(low, full[:HEAD_DIM], full[HEAD_DIM:])


def block_diag(packed, low):
    return jnp.concatenate(
        [jnp.where(low, packed, 0.0), jnp.where(low, 0.0, packed)], axis=0
    ).astype(BF16)


def pair_attention(p, gram_ref, sq_ref, sharp_ref, low, eye):
    gram = gram_ref[8 * p : 8 * p + 8].reshape(HEAD_DIM, 128)
    query_sq = half_sum(jnp.where(eye, sq_ref[p : p + 1, :], 0.0), low)
    query_norm = jnp.sqrt(query_sq + EPS)
    key_norm = jnp.sqrt(sq_ref[PAIRS + p : PAIRS + p + 1, :] + EPS)
    divisor = query_norm * key_norm
    sharp = jnp.where(low, sharp_ref[2 * p], sharp_ref[2 * p + 1])
    scores = sharp * gram / divisor
    exponent = jnp.exp(scores - half_max(scores, low))
    prob = exponent / half_sum(exponent, low)
    return prob, scores, divisor, sharp, query_norm, key_norm


def first_part(x_ref, gain_ref, w_ref, act_ref, mixed_ref, msg_ref):
    gain = gain_ref[...]

    def rows(i, _):
        at = ds(i * 32, 32)
        normed, _ = norm_parts(x_ref[at, :].astype(F32))
        act_ref[at, :] = (normed * gain).astype(BF16)
        return 0

    lax.fori_loop(0, TOK // 32, rows, 0)

    def mix(i, _):
        at = ds(i * 256, 256)
        mixed_ref[at, :] = dot(act_ref[at, :], w_ref[...], 1, 0).astype(BF16)
        return 0

    lax.fori_loop(0, TOK // 256, mix, 0)
    low = lane_low()
    sums = []
    for p in range(2 * PAIRS):
        sq = jnp.zeros((8, 128), F32)
        for i in range(0, TOK, 64):
            part = mixed_ref[i : i + 64, 128 * p : 128 * p + 128].astype(F32)
            sq = sq + (part * part).reshape(8, 8, 128).sum(0)
        sums.append(sq.sum(0, keepdims=True))
    sq = jnp.concatenate(sums, axis=0)
    for p in range(PAIRS):
        query = mixed_ref[:, 128 * p : 128 * p + 128]
        key = mixed_ref[:, D + 128 * p : D + 128 * p + 128]
        packed = pack_pair(dot(query, key, 0, 0), low)
        for b in range(8):
            msg_ref[8 * p + b, 0:8, :] = packed[8 * b : 8 * b + 8]
    for j in range(32):
        msg_ref[j, 8:16, :] = sq


def remote(src, dst, send, recv, **axes):
    return pltpu.make_async_remote_copy(
        src_ref=src, dst_ref=dst, send_sem=send, recv_sem=recv, device_id=axes, device_id_type=MESH_ID
    )


def greet_strips(n, me, barrier):
    def greet(k, _):
        pl.semaphore_signal(
            barrier, inc=1, device_id={"sp": lax.rem(me + k, n)}, device_id_type=MESH_ID
        )
        return 0

    lax.fori_loop(1, n, greet, 0)


def strip_sum(n, me, msg_ref, total_ref, got, mine, sems, rows, between):
    def first(k):
        j = lax.rem(me + k, n)
        return remote(msg_ref.at[j], got.at[k], sems[0].at[k], sems[1].at[k], sp=j)

    def second(k):
        j = lax.rem(me + k, n)
        return remote(mine, total_ref.at[me], sems[2].at[k], sems[3].at[k], sp=j)

    def start(copy):
        def go(k, _):
            copy(k).start()
            return 0

        lax.fori_loop(1, n, go, 0)

    start(first)
    between()

    def add(k, total):
        first(k).wait_recv()
        return total + got[k]

    total = lax.fori_loop(1, n, add, msg_ref[me])
    mine[...] = total[:rows]
    start(second)
    total_ref[me] = total[:rows]

    def finish(k, _):
        second(k).wait_recv()
        second(k).wait_send()
        first(k).wait_send()
        return 0

    return total, lambda: lax.fori_loop(1, n, finish, 0)


def gram_exchange(
    n, msg_ref, x_ref, up_ref, gram_ref, sq_ref, xe_ref, ue_ref, got, mine, s0, s1, s2, s3, hs, hr
):
    me = lax.axis_index("sp")
    below, above = lax.rem(me + 1, n), lax.rem(me + n - 1, n)
    barrier = pltpu.get_barrier_semaphore()
    greet_strips(n, me, barrier)
    pl.semaphore_wait(barrier, n - 1)
    halos = []
    for at, (src, dst) in enumerate(((x_ref, xe_ref), (up_ref, ue_ref))):
        halos.append(remote(src, dst.at[pl.ds(0, TOK)], hs.at[2 * at], hr.at[2 * at], sp=below))
        halos.append(
            remote(src, dst.at[pl.ds(2 * TOK, TOK)], hs.at[2 * at + 1], hr.at[2 * at + 1], sp=above)
        )

    def between():
        for copy in halos:
            copy.start()
        xe_ref[TOK : 2 * TOK, :] = x_ref[...]
        ue_ref[TOK : 2 * TOK, :] = up_ref[...]

    total, finish = strip_sum(n, me, msg_ref, gram_ref, got, mine, (s0, s1, s2, s3), 8, between)
    sq_ref[...] = total[8:]
    finish()
    for copy in halos:
        copy.wait()


def prob_exchange(n, msg_ref, prob_ref, small_ref, got, mine, s0, s1, s2, s3):
    me = lax.axis_index("sp")
    barrier = pltpu.get_barrier_semaphore()
    greet_strips(n, me, barrier)
    pl.semaphore_wait(barrier, n - 1)
    total, finish = strip_sum(
        n, me, msg_ref, prob_ref, got, mine, (s0, s1, s2, s3), 8, lambda: None
    )
    small_ref[...] = total[8:]
    finish()


def middle_part(
    n,
    sharp_ref,
    gram_ref,
    sq_ref,
    xe_ref,
    ue_ref,
    mixed_ref,
    w_ref,
    wo_ref,
    gain1_ref,
    gain2_ref,
    factor_ref,
    kern_ref,
    att_ref,
    dproj_ref,
    dval_ref,
    dres_ref,
    msg_ref,
    bd_s,
    ve_s,
    act_s,
    up_s,
    dh_s,
    hid_s,
    attrow_s,
    projrow_s,
    proj_s,
    normed_s,
    inv_s,
    dact_s,
    acc_s,
    datt_s,
):
    me = lax.axis_index("sp")
    first, last = me == 0, me == n - 1
    low, eye = lane_low(), eye_pair()
    for p in range(PAIRS):
        prob = pair_attention(p, gram_ref, sq_ref, sharp_ref, low, eye)[0]
        bd_s[p] = block_diag(prob, low)
    for ref, count in ((act_s, 6), (up_s, 6), (dh_s, 4), (hid_s, 4)):
        for r in range(count):
            ref[r, 0:8, :] = jnp.zeros((8, D), F32)
            ref[r, 264:272, :] = jnp.zeros((8, D), F32)
    acc_s[...] = jnp.zeros_like(acc_s)
    gain1, gain2 = gain1_ref[...], gain2_ref[...]
    factor0, factor1 = factor_ref[0:1, :], factor_ref[1:2, :]

    def outside(row):
        return ((row < 2) & first) | ((row > 3) & last)

    ve_s[TOK : 2 * TOK, :] = mixed_ref[:, 2 * D :]

    def halo_values(i, _):
        row = i + 2 * (i >= 2).astype(jnp.int32)

        def rows(c, _):
            at = ds(row * WIDTH + c * 32, 32)
            normed, _ = norm_parts(xe_ref[at, :].astype(F32))
            attrow_s[ds(c * 32, 32), :] = (normed * gain1).astype(BF16)
            return 0

        lax.fori_loop(0, WIDTH // 32, rows, 0)
        ve_s[ds(row * WIDTH, WIDTH), :] = dot(attrow_s[...], w_ref[:, 2 * D :], 1, 0).astype(BF16)
        return 0

    lax.fori_loop(0, 4, halo_values, 0)

    def forward_row(row, _):
        at_row = ds(row * WIDTH, WIDTH)
        for p in range(PAIRS):
            cols = slice(128 * p, 128 * p + 128)
            attrow_s[:, cols] = dot(ve_s[at_row, cols], bd_s[p], 1, 1).astype(BF16)
        projrow_s[...] = dot(attrow_s[...], wo_ref[...], 1, 0)
        keep = jnp.logical_not(outside(row))

        def rows(c, _):
            here = ds(c * 32, 32)
            u = xe_ref[ds(row * WIDTH + c * 32, 32), :].astype(F32) + factor0 * projrow_s[here, :]
            normed, inverse = norm_parts(u.astype(BF16).astype(F32))
            act = (normed * gain2).astype(BF16).astype(F32)
            act_s[row, ds(8 + c * 32, 32, 8), :] = jnp.where(keep, act, 0.0)

            @pl.when((row == 2) | (row == 3))
            def _():
                there = ds((row - 2) * WIDTH + c * 32, 32)
                att_ref[there, :] = attrow_s[here, :]
                proj_s[there, :] = projrow_s[here, :]
                normed_s[there, :] = normed
                inv_s[there, :] = jnp.broadcast_to(inverse, (32, 128))

            return 0

        lax.fori_loop(0, WIDTH // 32, rows, 0)
        return 0

    lax.fori_loop(0, 6, forward_row, 0)

    def upstream_rows(i, _):
        row, c = i // 4, lax.rem(i, 4)
        up = ue_ref[ds(row * WIDTH + c * 64, 64), :].astype(F32)
        up_s[row, ds(8 + c * 64, 64, 8), :] = jnp.where(outside(row), 0.0, up)
        return 0

    lax.fori_loop(0, 24, upstream_rows, 0)

    def taps(which, lanes, i, j):
        at = 9 * which + 3 * i + j
        return kern_ref[at : at + 1, lanes]

    def hidden_rows(idx, _):
        hrow, rest = idx // 16, lax.rem(idx, 16)
        lanes, c = ds((rest // 4) * 128, 128), lax.rem(rest, 4)
        win = ds(c * 64, 80, 8)
        near = [act_s[hrow + i, win, lanes] for i in range(3)]
        sums = []
        for j in range(3):
            sums.append(sum(taps(0, lanes, i, j) * near[i] for i in range(3)))
        h = (
            pltpu.roll(sums[0], 1, 0)[8:72]
            + sums[1][8:72]
            + pltpu.roll(sums[2], 79, 0)[8:72]
        )
        near = [up_s[hrow + 2 - i, win, lanes] for i in range(3)]
        sums = []
        scale = factor_ref[1:2, lanes]
        for j in range(3):
            sums.append(sum((taps(1, lanes, i, j) * scale) * near[i] for i in range(3)))
        d_hidden = (
            pltpu.roll(sums[0], 79, 0)[8:72]
            + sums[1][8:72]
            + pltpu.roll(sums[2], 1, 0)[8:72]
        )
        cumul = 0.5 * (1.0 + lax.erf(h * 0.7071067811865476))
        density = jnp.exp(-0.5 * h * h) * 0.3989422804014327
        there = ds(8 + c * 64, 64, 8)
        hid_s[hrow, there, lanes] = (h * cumul).astype(BF16).astype(F32)
        d_h = d_hidden * (cumul + h * density)
        dh_s[hrow, there, lanes] = jnp.where(outside(hrow + 1), 0.0, d_h)
        return 0

    lax.fori_loop(0, 64, hidden_rows, 0)

    def fold(v):
        return v.reshape(8, 8, 128).sum(0)

    def back_rows(idx, _):
        r, rest = idx // 16, lax.rem(idx, 16)
        lanes, c = ds((rest // 4) * 128, 128), lax.rem(rest, 4)
        win, mid = ds(c * 64, 80, 8), ds(8 + c * 64, 64, 8)
        near = [dh_s[r + 2 - i, win, lanes] for i in range(3)]
        sums = []
        for j in range(3):
            sums.append(sum(taps(0, lanes, i, j) * near[i] for i in range(3)))
        dact_s[ds(r * WIDTH + c * 64, 64), lanes] = (
            pltpu.roll(sums[0], 79, 0)[8:72]
            + sums[1][8:72]
            + pltpu.roll(sums[2], 1, 0)[8:72]
        )
        own = near[1]
        moved = [pltpu.roll(own, 79, 0)[8:72], own[8:72], pltpu.roll(own, 1, 0)[8:72]]
        for i in range(3):
            act = act_s[r + 1 + i, mid, lanes]
            for j in range(3):
                acc_s[3 * i + j, :, lanes] += fold(moved[j] * act)
        own = hid_s[r + 1, win, lanes]
        moved = [pltpu.roll(own, 1, 0)[8:72], own[8:72], pltpu.roll(own, 79, 0)[8:72]]
        for i in range(3):
            up = up_s[r + 3 - i, mid, lanes]
            for j in range(3):
                acc_s[9 + 3 * i + j, :, lanes] += fold(moved[j] * up)
        return 0

    lax.fori_loop(0, 32, back_rows, 0)

    def residual_rows(i, scale):
        row, c = i // 8, lax.rem(i, 8)
        at = ds(i * 32, 32)
        lnb = norm_back(dact_s[at, :], gain2, normed_s[at, :], inv_s[at, 0:1])
        d_res = up_s[row + 2, ds(8 + c * 32, 32, 8), :] + lnb
        dres_ref[at, :] = d_res
        dproj_ref[at, :] = (factor0 * d_res).astype(BF16)
        return scale + (proj_s[at, :] * d_res).reshape(4, 8, D).sum(0)

    scale_one = lax.fori_loop(0, TOK // 32, residual_rows, jnp.zeros((8, D), F32))
    lines = [acc_s[m].sum(0, keepdims=True) for m in range(18)]
    scale_two = sum(lines[9 + m] * kern_ref[9 + m : 10 + m, :] for m in range(9))
    lines = lines[:9] + [line * factor1 for line in lines[9:]]
    lines += [scale_one.sum(0, keepdims=True), scale_two]
    for j in range(32):
        msg_ref[j, 8:16, :] = jnp.zeros((8, 128), F32)
    for at in range(80):
        v, b = at // 4, at % 4
        msg_ref[at // 3, 8 + at % 3 : 9 + at % 3, :] = lines[v][:, 128 * b : 128 * b + 128]

    def attended_rows(i, _):
        at = ds(i * 256, 256)
        datt_s[at, :] = dot(dproj_ref[at, :], wo_ref[...], 1, 1).astype(BF16)
        for p in range(PAIRS):
            cols = slice(128 * p, 128 * p + 128)
            dval_ref[at, cols] = dot(datt_s[at, cols], bd_s[p], 1, 0).astype(BF16)
        return 0

    lax.fori_loop(0, 2, attended_rows, 0)
    for p in range(PAIRS):
        cols = slice(128 * p, 128 * p + 128)
        packed = pack_pair(dot(datt_s[:, cols], ve_s[TOK : 2 * TOK, cols], 0, 0), low)
        for b in range(8):
            msg_ref[8 * p + b, 0:8, :] = packed[8 * b : 8 * b + 8]


def last_part(
    sharp_ref,
    gram_ref,
    sq_ref,
    pg_ref,
    x_ref,
    act_ref,
    mixed_ref,
    w_ref,
    gain1_ref,
    att_ref,
    dproj_ref,
    dval_ref,
    dres_ref,
    out_ref,
    grads_ref,
    dmix_s,
    dact_s,
):
    low, eye = lane_low(), eye_pair()
    for p in range(PAIRS):
        prob, scores, divisor, sharp, query_norm, key_norm = pair_attention(
            p, gram_ref, sq_ref, sharp_ref, low, eye
        )
        pg = pg_ref[8 * p : 8 * p + 8].reshape(HEAD_DIM, 128)
        logit = prob * (pg - half_sum(prob * pg, low))
        bd = block_diag(logit * sharp / divisor, low)
        weighted = logit * scores
        d_qsq = -half_sum(weighted, low) / (2.0 * query_norm * query_norm)
        d_qsq = jnp.sum(jnp.where(eye, d_qsq, 0.0), 0, keepdims=True)
        d_ksq = -jnp.sum(weighted, 0, keepdims=True) / (2.0 * key_norm * key_norm)
        qc = slice(128 * p, 128 * p + 128)
        kc = slice(D + 128 * p, D + 128 * p + 128)
        for i in range(0, TOK, 256):
            at = slice(i, i + 256)
            query, key = mixed_ref[at, qc], mixed_ref[at, kc]
            dmix_s[at, qc] = (dot(key, bd, 1, 1) + 2.0 * d_qsq * query.astype(F32)).astype(BF16)
            dmix_s[at, kc] = (dot(query, bd, 1, 0) + 2.0 * d_ksq * key.astype(F32)).astype(BF16)
    dmix_s[:, 2 * D :] = dval_ref[...]

    def inputs(i, _):
        at = ds(i * 256, 256)
        dact_s[at, :] = dot(dmix_s[at, :], w_ref[...], 1, 1)
        return 0

    lax.fori_loop(0, 2, inputs, 0)
    gain1 = gain1_ref[...]

    def rows(i, _):
        at = ds(i * 32, 32)
        normed, inverse = norm_parts(x_ref[at, :].astype(F32))
        lnb = norm_back(dact_s[at, :], gain1, normed, inverse)
        out_ref[at, :] = (dres_ref[at, :] + lnb).astype(BF16)
        return 0

    lax.fori_loop(0, TOK // 32, rows, 0)
    for half in range(2):
        for block in range(4):
            cols = slice(512 * block, 512 * block + 512)
            left = act_ref if block < 3 else att_ref
            right = dmix_s[:, cols] if block < 3 else dproj_ref[...]
            g = dot(left[:, 256 * half : 256 * half + 256], right, 0, 0).astype(BF16)
            for r in range(4):
                rep = 4 * half + r
                grads_ref[rep % 2, rep // 2, :, cols] = g[64 * r : 64 * r + 64]


def grad_exchange(
    n,
    grads_ref,
    small_ref,
    gq_ref,
    gp_ref,
    conv_ref,
    scale_ref,
    rb1,
    sb2,
    rb2,
    acc,
    sb3,
    rb3,
    fin,
    rb4,
    srb,
    sfin,
    sout,
    a0,
    a1,
    b0,
    b1,
    c0,
    c1,
    d0,
    d1,
    e0,
    e1,
    f0,
    f1,
):
    me = lax.axis_index("sp")
    rep = lax.axis_index("rep")
    reps = 8
    y, core = rep // 2, lax.rem(rep, 2)
    barrier = pltpu.get_barrier_semaphore()
    greet_strips(n, me, barrier)
    for k in range(1, reps):
        pl.semaphore_signal(
            barrier, inc=1, device_id={"rep": lax.rem(rep + k, reps)}, device_id_type=MESH_ID
        )
    pl.semaphore_wait(barrier, n - 1 + reps - 1)
    partner = 2 * y + 1 - core
    pair = []
    for k in range(4):
        there = lax.rem(y + 1 + k, 4)
        pair.append(
            remote(grads_ref.at[1 - core, there], rb1.at[k], a0.at[k], a1.at[k], rep=partner)
        )
    for copy in pair:
        copy.start()
    smalls = []
    for k in range(1, reps):
        smalls.append(
            remote(small_ref, srb.at[rep], e0.at[k], e1.at[k], rep=lax.rem(rep + k, reps))
        )
    for copy in smalls:
        copy.start()
    srb[rep] = small_ref[...]
    columns = []
    for k in range(3):
        there = lax.rem(y + 1 + k, 4)
        pair[k].wait_recv()

        def add(i, _, k=k, there=there):
            at = ds(i * 16, 16)
            sb2[k, at, :] = (
                grads_ref[core, there, at, :].astype(F32) + rb1[k, at, :].astype(F32)
            ).astype(BF16)
            return 0

        lax.fori_loop(0, 4, add, 0)
        copy = remote(sb2.at[k], rb2.at[k], b0.at[k], b1.at[k], rep=2 * there + core)
        copy.start()
        columns.append(copy)
    pair[3].wait_recv()

    def own(i, _):
        at = ds(i * 16, 16)
        acc[at, :] = grads_ref[core, y, at, :].astype(F32) + rb1[3, at, :].astype(F32)
        return 0

    lax.fori_loop(0, 4, own, 0)
    for copy in columns:
        copy.wait_recv()
    for j in range(n):
        rows, cols = slice(32 * (j // 16), 32 * (j // 16) + 32), slice(128 * (j % 16), 128 * (j % 16) + 128)
        total = acc[rows, cols]
        for k in range(3):
            total = total + rb2[k, rows, cols].astype(F32)
        sb3[j] = total.astype(BF16)

    def third(k):
        j = lax.rem(me + k, n)
        return remote(sb3.at[j], rb3.at[k], c0.at[k], c1.at[k], sp=j)

    def fourth(k):
        return remote(fin, rb4.at[me], d0.at[k], d1.at[k], sp=lax.rem(me + k, n))

    def fifth(k):
        return remote(sfin, sout.at[me], f0.at[k], f1.at[k], sp=lax.rem(me + k, n))

    def start_third(k, _):
        third(k).start()
        return 0

    lax.fori_loop(1, n, start_third, 0)
    for copy in smalls:
        copy.wait_recv()
    total = srb[0]
    for k in range(1, reps):
        total = total + srb[k]
    sfin[...] = total
    sout[me] = total

    def start_fifth(k, _):
        fifth(k).start()
        return 0

    lax.fori_loop(1, n, start_fifth, 0)

    def add_third(k, total):
        third(k).wait_recv()
        return total + rb3[k].astype(F32)

    total = lax.fori_loop(1, n, add_third, sb3[me].astype(F32)).astype(BF16)
    fin[...] = total
    rb4[me] = total

    def start_fourth(k, _):
        fourth(k).start()
        return 0

    lax.fori_loop(1, n, start_fourth, 0)

    def finish(k, _):
        fourth(k).wait_recv()
        fifth(k).wait_recv()
        fourth(k).wait_send()
        fifth(k).wait_send()
        third(k).wait_send()
        return 0

    lax.fori_loop(1, n, finish, 0)
    for j in range(n):
        rows, at = slice(32 * (j // 16), 32 * (j // 16) + 32), 128 * (j % 16)
        if at < 3 * D:
            gq_ref[rows, at : at + 128] = rb4[j].astype(F32)
        else:
            gp_ref[rows, at - 3 * D : at - 3 * D + 128] = rb4[j].astype(F32)
    for at in range(80):
        v, b = at // 4, at % 4
        line = sout[at // 3, at % 3 : at % 3 + 1, :]
        if v < 18:
            conv_ref[v : v + 1, 128 * b : 128 * b + 128] = line
        else:
            scale_ref[v - 18 : v - 17, 128 * b : 128 * b + 128] = line
    for copy in pair + smalls + columns:
        copy.wait_send()


def call(body, name, outs, scratch, args, smem=0, collective=None):
    params = dict(vmem_limit_bytes=LIMIT)
    if collective is not None:
        params.update(collective_id=collective, has_side_effects=True)
    specs = [pl.BlockSpec(memory_space=pltpu.SMEM)] * smem
    specs += [pl.BlockSpec(memory_space=VMEM)] * (len(args) - smem)
    return pl.pallas_call(
        body,
        name=name,
        out_shape=[jax.ShapeDtypeStruct(s, t) for s, t in outs],
        in_specs=specs,
        out_specs=[pl.BlockSpec(memory_space=VMEM)] * len(outs),
        scratch_shapes=scratch,
        compiler_params=pltpu.CompilerParams(**params),
    )(*args)


def dma(*counts):
    return [pltpu.SemaphoreType.DMA((c,)) for c in counts]


def shards(n, x, up, gain1, w, sharp, wo, factors, gain2, kernels):
    x = x.reshape(TOK, D)
    up = up.reshape(TOK, D)
    gain1, gain2 = gain1.reshape(1, D), gain2.reshape(1, D)
    kern = kernels.reshape(18, D)
    act, mixed, msg = call(
        first_part,
        "first_part",
        [((TOK, D), BF16), ((TOK, 3 * D), BF16), ((n, 16, 128), F32)],
        [],
        (x, gain1, w),
    )
    gram, sq, xe, ue = call(
        functools.partial(gram_exchange, n),
        "gram_exchange",
        [((n, 8, 128), F32), ((8, 128), F32), ((3 * TOK, D), BF16), ((3 * TOK, D), BF16)],
        [VMEM((n, 16, 128), F32), VMEM((8, 128), F32)] + dma(n, n, n, n, 4, 4),
        (msg, x, up),
        collective=0,
    )
    att, dproj, dval, dres, msg = call(
        functools.partial(middle_part, n),
        "middle_part",
        [((TOK, D), BF16)] * 3 + [((TOK, D), F32), ((n, 16, 128), F32)],
        [
            VMEM((PAIRS, 128, 128), BF16),
            VMEM((3 * TOK, D), BF16),
            VMEM((6, 272, D), F32),
            VMEM((6, 272, D), F32),
            VMEM((4, 272, D), F32),
            VMEM((4, 272, D), F32),
            VMEM((WIDTH, D), BF16),
            VMEM((WIDTH, D), F32),
            VMEM((TOK, D), F32),
            VMEM((TOK, D), F32),
            VMEM((TOK, 128), F32),
            VMEM((TOK, D), F32),
            VMEM((18, 8, D), F32),
            VMEM((TOK, D), BF16),
        ],
        (sharp, gram, sq, xe, ue, mixed, w, wo, gain1, gain2, factors, kern),
        smem=1,
    )
    pg, small = call(
        functools.partial(prob_exchange, n),
        "prob_exchange",
        [((n, 8, 128), F32), ((8, 128), F32)],
        [VMEM((n, 16, 128), F32), VMEM((8, 128), F32)] + dma(n, n, n, n),
        (msg,),
        collective=1,
    )
    out, grads = call(
        last_part,
        "last_part",
        [((TOK, D), BF16), ((2, 4, 64, 2048), BF16)],
        [VMEM((TOK, 3 * D), BF16), VMEM((TOK, D), F32)],
        (sharp, gram, sq, pg, x, act, mixed, w, gain1, att, dproj, dval, dres),
        smem=1,
    )
    gq, gp, conv, scale = call(
        functools.partial(grad_exchange, n),
        "grad_exchange",
        [((64, 3 * D), F32), ((64, D), F32), ((18, D), F32), ((2, D), F32)],
        [
            VMEM((4, 64, 2048), BF16),
            VMEM((3, 64, 2048), BF16),
            VMEM((3, 64, 2048), BF16),
            VMEM((64, 2048), F32),
            VMEM((n, 32, 128), BF16),
            VMEM((n, 32, 128), BF16),
            VMEM((32, 128), BF16),
            VMEM((n, 32, 128), BF16),
            VMEM((8, 8, 128), F32),
            VMEM((8, 128), F32),
            VMEM((n, 8, 128), F32),
        ]
        + dma(4, 4, 3, 3, n, n, n, n, 8, 8, n, n),
        (grads, small),
        collective=2,
    )
    return out.reshape(1, 2, WIDTH, D), gq, gp, conv.reshape(2, 3, 3, D), scale


def solution(mesh):
    tokens = P("rep", "sp", None, None)
    in_specs = (tokens, tokens, P(), P(), P(), P(), P(), P(), P())
    out_specs = (tokens, P("rep", None), P("rep", None), P(), P())
    return jax.shard_map(
        functools.partial(shards, mesh.shape["sp"]),
        mesh=mesh,
        in_specs=in_specs,
        out_specs=out_specs,
        check_vma=False,
    )
```

time: 311 us -> 180 us (0.58); the launches traced: 307 us -> 179 us
  Pallas kernels: 0 us -> 171 us
  starting transfers between devices: 106 us -> 0 us
  waiting for transfers between devices: 69.9 us -> 0 us
  other arithmetic: 56.6 us -> 0 us
  local copies, waits for them, and re-layouts: 43.8 us -> 7.49 us
  matrix products: 18.4 us -> 0 us
  blocking collectives: 10.4 us -> 0 us
    pallas_call x0 -> x6, Pallas kernels: none -> 171 us  [call(): pl.pallas_call(body, name=name, out_shape=[jax.ShapeDtypeStruct(s, t) for...]
    all_to_all x11 -> x0, starting transfers between devices: 84.1 us -> none  [the longest x4 42.9 us: sum_at_owner(): lax.all_to_all(tiles, axis, split_axis=0, concat_axis=0, tiled=True)]
    all_to_all x11 -> x0, waiting for transfers between devices: 65.9 us -> none  [the longest x2 27.4 us: sum_by_axis(): return jnp.sum(lax.all_to_all(own, far, 0, 0, tiled=True), axis=0)]
    reduce_sum x20 -> x0, other arithmetic: 27.5 us -> none  [the longest x5 6.2 us: sum_at_owner(): return arrived.sum(axis=0)]
    ppermute x8 -> x0, starting transfers between devices: 21.7 us -> none  [the longest x4 12.3 us: shifted_2(): lax.ppermute(value, axis, [(source, source + steps) for source in range(l...]
    dot_general x12 -> x0, matrix products: 18.4 us -> none  [the longest x1 2.67 us: shards(): lax.dot_general(d_mixed, triple_mapping_matrix, (((1,), (1,)), ((), ())),...]
    slice x23 -> x0, local copies, waits for them, and re-layouts: 17.6 us -> none  [the longest x5 5.59 us: packed_total(): total[b:e].reshape(a.shape)]
    all_to_all x1 -> x0, blocking collectives: 10.4 us -> none  [sum_at_owner(): lax.all_to_all(tiles, axis, split_axis=0, concat_axis=0, tiled=True)]
  transfers between devices with their start and end apart: 19 -> 0, of which waited for: 10 -> 0; matrix products, arithmetic and copies ran while one was open for 26% -> 0% of each run, Pallas kernels for 0% -> 0%
where the time goes in v1:
time: 180 us; the launch traced here: 179 us
  Pallas kernels  171 us (95%)
  local copies, waits for them, and re-layouts  7.49 us (4%)
    pallas_call x6, Pallas kernels, call(): pl.pallas_call(body, name=name, out_shape=[jax.ShapeDtypeStruct(s, t) for...  171 us
    unnamed x5, local copies, waits for them, and re-layouts  6.03 us

profile of v1, /device:TPU:1, one launch (start us, length us, event | category | flops | bytes accessed | tf_op | source)
XLA Modules:
  0.0 179.3 jit_solution(16604205279854160616)
XLA Ops:
  0.6 0.8 copy.16
  1.4 0.6 reshape.35.kern_ref
  2.1 6.8 %first_part.1 = (bf16[512,512]{1,0:T(8,128)(2,1)}, bf16[512,1536]{1,0:T(8,128)(2,1)}, f32[32,16,128]{2,1,0:T(8,128)}) custom-call(bf16[512,512]{1,0:T(8,128)(2,1)} %bitcast.5, f32[1,512]{1,0:T(1,128)} %bitcast.9, bf16[512,1536]{1,0:T(8,128)(2,1)} %w_ref.5), custom_call_target="tpu_custom_call" | custom-call | tf_op jit(solution)/shard_map/first_part/pallas_call | solution.py:668
  8.9 47.0 %gram_exchange.1 = (f32[32,8,128]{2,1,0:T(8,128)}, f32[8,128]{1,0:T(8,128)}, bf16[1536,512]{1,0:T(8,128)(2,1)}, bf16[1536,512]{1,0:T(8,128)(2,1)}) custom-call(f32[32,16,128]{2,1,0:T(8,128)} %get-tuple-element.25.msg_ref, bf16[512,512]{1,0:T(8,128)(2,1)} %bitcast.6, bf16[512,512]{1,0:T(8,128)(2,1)} %bitcast.8), custom_call_target="tpu_custom_call" | custom-call | tf_op jit(solution)/shard_map/gram_exchange/pallas_call | solution.py:668
  55.9 36.1 %middle_part.1 = (bf16[512,512]{1,0:T(8,128)(2,1)}, bf16[512,512]{1,0:T(8,128)(2,1)}, bf16[512,512]{1,0:T(8,128)(2,1)}, f32[512,512]{1,0:T(8,128)}, f32[32,16,128]{2,1,0:T(8,128)}) custom-call(f32[8]{0:T(128)} %sharp_ref.3, f32[32,8,128]{2,1,0:T(8,128)} %get-tuple-element.26.gram_ref, f32[8,128]{1,0:T(8,128)} %get-tuple-element.27.sq_ref, ...), custom_call_target="tpu_custom_call" | custom-call | tf_op jit(solution)/shard_map/middle_part/pallas_call | solution.py:668
  92.0 22.5 %prob_exchange.1 = (f32[32,8,128]{2,1,0:T(8,128)}, f32[8,128]{1,0:T(8,128)}) custom-call(f32[32,16,128]{2,1,0:T(8,128)} %get-tuple-element.31.msg_ref), custom_call_target="tpu_custom_call" | custom-call | tf_op jit(solution)/shard_map/prob_exchange/pallas_call | solution.py:668
  114.5 12.2 %last_part.1 = (bf16[512,512]{1,0:T(8,128)(2,1)}, bf16[2,4,64,2048]{3,2,1,0:T(8,128)(2,1)}) custom-call(f32[8]{0:T(128)} %sharp_ref.3, f32[32,8,128]{2,1,0:T(8,128)} %get-tuple-element.26.gram_ref, f32[8,128]{1,0:T(8,128)} %get-tuple-element.27.sq_ref, f32[32,8,128]{2,1,0:T(8,128)} %get-tuple-element.32.pg_ref, bf16[512,512]{1,0:T(8,128)(2,1)} %bitcast.7, ...), custom_call_target="tpu_custom_call" | custom-call | tf_op jit(solution)/shard_map/last_part/pallas_call | solution.py:668
  126.7 46.5 %grad_exchange.1 = (f32[64,1536]{1,0:T(8,128)}, f32[64,512]{1,0:T(8,128)}, f32[18,512]{1,0:T(8,128)}, f32[2,512]{1,0:T(2,128)}) custom-call(bf16[2,4,64,2048]{3,2,1,0:T(8,128)(2,1)} %get-tuple-element.39.grads_ref, f32[8,128]{1,0:T(8,128)} %get-tuple-element.40.small_ref), custom_call_target="tpu_custom_call" | custom-call | tf_op jit(solution)/shard_map/grad_exchange/pallas_call | solution.py:668
  173.2 0.8 reshape.37
  174.1 0.6 copy.17
  174.7 1.8 copy.21
  176.5 1.6 copy.22
  178.0 1.3 copy.23

commit v2 on v0

v2 whole, which is shorter than its diff:
```python
import functools

import jax
import jax.numpy as jnp
from jax import lax
from jax.experimental import pallas as pl
from jax.experimental.pallas import tpu as pltpu
from jax.sharding import PartitionSpec as P

D = 512
HEADS = 8
HEAD_DIM = 64
WIDTH = 256
EPS = 1e-06
F32 = jnp.float32
BF16 = jnp.bfloat16
TOK = 512
PAIRS = 4
VMEM = pltpu.VMEM
MESH_ID = pl.DeviceIdType.MESH
LIMIT = 60 * 1024 * 1024


def dot(a, b, ca, cb):
    return lax.dot_general(a, b, (((ca,), (cb,)), ((), ())), preferred_element_type=F32)


def ds(start, size, multiple=None):
    return pl.ds(pl.multiple_of(start, multiple or size), size)


def norm_parts(u):
    centre = jnp.mean(u, -1, keepdims=True)
    centred = u - centre
    inverse = lax.rsqrt(jnp.mean(centred * centred, -1, keepdims=True) + EPS)
    return centred * inverse, inverse


def norm_back(upstream, gain, normed, inverse):
    scaled = upstream * gain
    return inverse * (
        scaled
        - jnp.mean(scaled, -1, keepdims=True)
        - normed * jnp.mean(scaled * normed, -1, keepdims=True)
    )


def lane_low():
    return lax.broadcasted_iota(jnp.int32, (HEAD_DIM, 128), 1) < HEAD_DIM


def eye_pair():
    lane = lax.broadcasted_iota(jnp.int32, (HEAD_DIM, 128), 1)
    row = lax.broadcasted_iota(jnp.int32, (HEAD_DIM, 128), 0)
    return (lane == row) | (lane == row + HEAD_DIM)


def half_sum(v, low):
    left = jnp.sum(jnp.where(low, v, 0.0), -1, keepdims=True)
    right = jnp.sum(jnp.where(low, 0.0, v), -1, keepdims=True)
    return jnp.where(low, left, right)


def half_max(v, low):
    left = jnp.max(jnp.where(low, v, -jnp.inf), -1, keepdims=True)
    right = jnp.max(jnp.where(low, -jnp.inf, v), -1, keepdims=True)
    return jnp.where(low, left, right)


def pack_pair(full, low):
    return jnp.where(low, full[:HEAD_DIM], full[HEAD_DIM:])


def block_diag(packed, low):
    return jnp.concatenate(
        [jnp.where(low, packed, 0.0), jnp.where(low, 0.0, packed)], axis=0
    ).astype(BF16)


def pair_attention(p, gram_ref, sq_ref, sharp_ref, low, eye):
    gram = gram_ref[8 * p : 8 * p + 8].reshape(HEAD_DIM, 128)
    query_sq = half_sum(jnp.where(eye, sq_ref[p : p + 1, :], 0.0), low)
    query_norm = jnp.sqrt(query_sq + EPS)
    key_norm = jnp.sqrt(sq_ref[PAIRS + p : PAIRS + p + 1, :] + EPS)
    divisor = query_norm * key_norm
    sharp = jnp.where(low, sharp_ref[2 * p], sharp_ref[2 * p + 1])
    scores = sharp * gram / divisor
    exponent = jnp.exp(scores - half_max(scores, low))
    prob = exponent / half_sum(exponent, low)
    return prob, scores, divisor, sharp, query_norm, key_norm


def remote(src, dst, sems, at, **axes):
    return pltpu.make_async_remote_copy(
        src_ref=src,
        dst_ref=dst,
        send_sem=sems.at[0, at],
        recv_sem=sems.at[1, at],
        device_id=axes,
        device_id_type=MESH_ID,
    )


def loop(count, step, first=0):
    def go(i, _):
        step(i)
        return 0

    lax.fori_loop(first, count, go, 0)


def fold(v):
    return v.reshape(-1, 8, v.shape[-1]).sum(0)


def chunk(j):
    return slice(16 * (j // 8), 16 * (j // 8) + 16), slice(128 * (j % 8), 128 * (j % 8) + 128)


def layer(
    n,
    sharp_ref,
    x_ref,
    up_ref,
    gain1_ref,
    w_ref,
    wo_ref,
    factor_ref,
    gain2_ref,
    kern4_ref,
    out_ref,
    grads_ref,
    small_ref,
    act1_s,
    mixed_s,
    gmsg,
    ggot,
    gmine,
    gram_s,
    sq_s,
    kern_ref,
    up_halo,
    act_halo,
    dh_halo,
    act_edge,
    dh_edge,
    act_s,
    up_s,
    dh_s,
    hid_s,
    dhid_s,
    bd_s,
    att_s,
    proj_s,
    normed_s,
    inv_s,
    dact_s,
    acc_s,
    dproj_s,
    dres_s,
    datt_s,
    dmix_s,
    pmsg,
    pgot,
    pmine,
    pg_s,
    gl,
    rb1,
    sb2,
    rb2,
    acc2,
    sb3,
    rb3,
    fin,
    srb,
    ssend,
    sfin,
    s_g1,
    s_g2,
    s_p1,
    s_p2,
    s_up,
    s_act,
    s_dh,
    s_pair,
    s_col,
    s_third,
    s_fourth,
    s_small,
    s_fifth,
):
    me, rep = lax.axis_index("sp"), lax.axis_index("rep")
    reps = 8
    y, core = rep // 2, lax.rem(rep, 2)
    barrier = pltpu.get_barrier_semaphore()

    def greet(k):
        pl.semaphore_signal(
            barrier, inc=1, device_id={"sp": lax.rem(me + k, n)}, device_id_type=MESH_ID
        )

    loop(n, greet, 1)
    for k in range(1, reps):
        pl.semaphore_signal(
            barrier, inc=1, device_id={"rep": lax.rem(rep + k, reps)}, device_id_type=MESH_ID
        )
    low, eye = lane_low(), eye_pair()
    gain1, gain2 = gain1_ref[...], gain2_ref[...]
    factor0, factor1 = factor_ref[0:1, :], factor_ref[1:2, :]

    def to_above(src, halo, sems):
        return remote(src, halo.at[1], sems, 0, sp=me - 1)

    def to_below(src, halo, sems):
        return remote(src, halo.at[0], sems, 1, sp=me + 1)

    def send_above(src, halo, sems):
        @pl.when(me > 0)
        def _():
            to_above(src, halo, sems).start()

    def send_below(src, halo, sems):
        @pl.when(me < n - 1)
        def _():
            to_below(src, halo, sems).start()

    def halos_in(src, halo, sems):
        @pl.when(me > 0)
        def _():
            to_below(src, halo, sems).wait_recv()

        @pl.when(me == 0)
        def _():
            halo[0] = jnp.zeros((WIDTH, D), BF16)

        @pl.when(me < n - 1)
        def _():
            to_above(src, halo, sems).wait_recv()

        @pl.when(me == n - 1)
        def _():
            halo[1] = jnp.zeros((WIDTH, D), BF16)

    def halos_sent(src, halo, sems):
        @pl.when(me > 0)
        def _():
            to_above(src, halo, sems).wait_send()

        @pl.when(me < n - 1)
        def _():
            to_below(src, halo, sems).wait_send()

    def spread(halo, target):
        def rows(i):
            side, c = i // 4, lax.rem(i, 4)
            target[3 * side, ds(8 + c * 64, 64, 8), :] = halo[side, ds(c * 64, 64), :].astype(F32)

        loop(8, rows)

    def part_to(msg, got, sems):
        def copy(k):
            j = lax.rem(me + k, n)
            return remote(msg.at[j], got.at[k], sems, k, sp=j)

        return copy

    def part_from(mine, total, sems):
        return lambda k: remote(mine, total.at[me], sems, k, sp=lax.rem(me + k, n))

    def start_all(copy):
        loop(n, lambda k: copy(k).start(), 1)

    def add_all(copy, got, own):
        def add(k, total):
            copy(k).wait_recv()
            return total + got[k].astype(F32)

        return lax.fori_loop(1, n, add, own)

    def received(copy):
        loop(n, lambda k: copy(k).wait_recv(), 1)

    def sent(copy):
        loop(n, lambda k: copy(k).wait_send(), 1)

    def norm_one(i):
        at = ds(i * 32, 32)
        normed, _ = norm_parts(x_ref[at, :].astype(F32))
        act1_s[at, :] = (normed * gain1).astype(BF16)

    loop(TOK // 32, norm_one)

    def mix(i):
        at = ds(i * 256, 256)
        mixed_s[at, :] = dot(act1_s[at, :], w_ref[...], 1, 0).astype(BF16)

    loop(2, mix)
    lines = []
    for p in range(2 * PAIRS):
        sq = jnp.zeros((8, 128), F32)
        for i in range(0, TOK, 64):
            part = mixed_s[i : i + 64, 128 * p : 128 * p + 128].astype(F32)
            sq = sq + fold(part * part)
        lines.append(sq.sum(0, keepdims=True))
    sq = jnp.concatenate(lines, axis=0)
    for p in range(PAIRS):
        query = mixed_s[:, 128 * p : 128 * p + 128]
        key = mixed_s[:, D + 128 * p : D + 128 * p + 128]
        packed = pack_pair(dot(query, key, 0, 0), low)
        for b in range(8):
            gmsg[8 * p + b, 0:8, :] = packed[8 * b : 8 * b + 8]
    for j in range(n):
        gmsg[j, 8:16, :] = sq
    pl.semaphore_wait(barrier, n - 1 + reps - 1)
    gram_out, gram_back = part_to(gmsg, ggot, s_g1), part_from(gmine, gram_s, s_g2)
    start_all(gram_out)
    up_row = [up_ref.at[pl.ds(0, WIDTH)], up_ref.at[pl.ds(WIDTH, WIDTH)]]
    send_above(up_row[0], up_halo, s_up)
    send_below(up_row[1], up_halo, s_up)

    for at in range(18):
        kern_ref[at : at + 1, :] = kern4_ref[at // 9, (at // 3) % 3, at % 3 : at % 3 + 1, :]
    for ref, count in ((act_s, 4), (up_s, 4), (dh_s, 4), (hid_s, 2)):
        for r in range(count):
            ref[r, 0:8, :] = jnp.zeros((8, D), F32)
            ref[r, 264:272, :] = jnp.zeros((8, D), F32)
    acc_s[...] = jnp.zeros_like(acc_s)

    def upstream_rows(i):
        row, c = i // 4, lax.rem(i, 4)
        up_s[row + 1, ds(8 + c * 64, 64, 8), :] = up_ref[ds(i * 64, 64), :].astype(F32)

    loop(8, upstream_rows)
    total = add_all(gram_out, ggot, gmsg[me])
    gmine[...] = total[:8]
    start_all(gram_back)
    gram_s[me] = total[:8]
    sq_s[...] = total[8:]
    received(gram_back)

    for p in range(PAIRS):
        prob = pair_attention(p, gram_s, sq_s, sharp_ref, low, eye)[0]
        bd_s[p] = block_diag(prob, low)
    for row in range(2):
        at_row = slice(row * WIDTH, row * WIDTH + WIDTH)
        for p in range(PAIRS):
            cols = slice(128 * p, 128 * p + 128)
            value = mixed_s[at_row, 2 * D + 128 * p : 2 * D + 128 * p + 128]
            att_s[at_row, cols] = dot(value, bd_s[p], 1, 1).astype(BF16)
        proj_s[at_row, :] = dot(att_s[at_row, :], wo_ref[...], 1, 0)

        def norm_two(c, row=row):
            at = ds(row * WIDTH + c * 32, 32)
            u = x_ref[at, :].astype(F32) + factor0 * proj_s[at, :]
            normed, inverse = norm_parts(u.astype(BF16).astype(F32))
            act = (normed * gain2).astype(BF16)
            act_edge[row, ds(c * 32, 32), :] = act
            act_s[row + 1, ds(8 + c * 32, 32, 8), :] = act.astype(F32)
            normed_s[at, :] = normed
            inv_s[at, :] = jnp.broadcast_to(inverse, (32, 128))

        loop(WIDTH // 32, norm_two)
        if row == 0:
            send_above(act_edge.at[0], act_halo, s_act)
        else:
            send_below(act_edge.at[1], act_halo, s_act)

    def taps(which, lanes, i, j):
        at = 9 * which + 3 * i + j
        return kern_ref[at : at + 1, lanes]

    def place(idx):
        return ds((idx // 4) * 128, 128), lax.rem(idx, 4)

    def forth(sums):
        return pltpu.roll(sums[0], 1, 0)[8:72] + sums[1][8:72] + pltpu.roll(sums[2], 79, 0)[8:72]

    def back(sums):
        return pltpu.roll(sums[0], 79, 0)[8:72] + sums[1][8:72] + pltpu.roll(sums[2], 1, 0)[8:72]

    halos_in(up_row[0], up_halo, s_up)
    spread(up_halo, up_s)

    def hidden_grads(idx):
        r = idx // 16
        lanes, c = place(lax.rem(idx, 16))
        win = ds(c * 64, 80, 8)
        near = [up_s[r + 2 - i, win, lanes] for i in range(3)]
        scale = factor_ref[1:2, lanes]
        sums = [sum((taps(1, lanes, i, j) * scale) * near[i] for i in range(3)) for j in range(3)]
        dhid_s[ds(r * WIDTH + c * 64, 64), lanes] = back(sums)

    loop(32, hidden_grads)
    halos_in(act_edge.at[0], act_halo, s_act)
    spread(act_halo, act_s)
    for r in range(2):

        def hidden_row(idx, r=r):
            lanes, c = place(idx)
            win, mid = ds(c * 64, 80, 8), ds(8 + c * 64, 64, 8)
            near = [act_s[r + i, win, lanes] for i in range(3)]
            h = forth([sum(taps(0, lanes, i, j) * near[i] for i in range(3)) for j in range(3)])
            cumul = 0.5 * (1.0 + lax.erf(h * 0.7071067811865476))
            density = jnp.exp(-0.5 * h * h) * 0.3989422804014327
            hid_s[r, mid, lanes] = (h * cumul).astype(BF16).astype(F32)
            d_h = dhid_s[ds(r * WIDTH + c * 64, 64), lanes] * (cumul + h * density)
            dh_s[r + 1, mid, lanes] = d_h
            dh_edge[r, ds(c * 64, 64), lanes] = d_h.astype(BF16)

        loop(16, hidden_row)
        if r == 0:
            send_above(dh_edge.at[0], dh_halo, s_dh)
        else:
            send_below(dh_edge.at[1], dh_halo, s_dh)

    def kernel_grads(idx):
        r = idx // 16
        lanes, c = place(lax.rem(idx, 16))
        win, mid = ds(c * 64, 80, 8), ds(8 + c * 64, 64, 8)
        own = dh_s[r + 1, win, lanes]
        moved = [pltpu.roll(own, 79, 0)[8:72], own[8:72], pltpu.roll(own, 1, 0)[8:72]]
        for i in range(3):
            act = act_s[r + i, mid, lanes]
            for j in range(3):
                acc_s[3 * i + j, :, lanes] += fold(moved[j] * act)
        own = hid_s[r, win, lanes]
        moved = [pltpu.roll(own, 1, 0)[8:72], own[8:72], pltpu.roll(own, 79, 0)[8:72]]
        for i in range(3):
            up = up_s[r + 2 - i, mid, lanes]
            for j in range(3):
                acc_s[9 + 3 * i + j, :, lanes] += fold(moved[j] * up)

    loop(32, kernel_grads)
    halos_in(dh_edge.at[0], dh_halo, s_dh)
    spread(dh_halo, dh_s)

    def act_grads(idx):
        r = idx // 16
        lanes, c = place(lax.rem(idx, 16))
        win = ds(c * 64, 80, 8)
        near = [dh_s[r + 2 - i, win, lanes] for i in range(3)]
        sums = [sum(taps(0, lanes, i, j) * near[i] for i in range(3)) for j in range(3)]
        dact_s[ds(r * WIDTH + c * 64, 64), lanes] = back(sums)

    loop(32, act_grads)

    def residual_rows(i, scale):
        row, c = i // 8, lax.rem(i, 8)
        at = ds(i * 32, 32)
        lnb = norm_back(dact_s[at, :], gain2, normed_s[at, :], inv_s[at, 0:1])
        d_res = up_s[row + 1, ds(8 + c * 32, 32, 8), :] + lnb
        dres_s[at, :] = d_res
        dproj_s[at, :] = (factor0 * d_res).astype(BF16)
        return scale + fold(proj_s[at, :] * d_res)

    scale_one = lax.fori_loop(0, TOK // 32, residual_rows, jnp.zeros((8, D), F32))

    def attended_rows(i):
        at = ds(i * 256, 256)
        datt_s[at, :] = dot(dproj_s[at, :], wo_ref[...], 1, 1).astype(BF16)

    loop(2, attended_rows)
    for p in range(PAIRS):
        cols = slice(128 * p, 128 * p + 128)
        value = mixed_s[:, 2 * D + 128 * p : 2 * D + 128 * p + 128]
        packed = pack_pair(dot(datt_s[:, cols], value, 0, 0), low)
        for b in range(8):
            pmsg[8 * p + b, 0:8, :] = packed[8 * b : 8 * b + 8]
    lines = [acc_s[m].sum(0, keepdims=True) for m in range(18)]
    scale_two = sum(lines[9 + m] * kern_ref[9 + m : 10 + m, :] for m in range(9))
    lines = lines[:9] + [line * factor1 for line in lines[9:]]
    lines += [scale_one.sum(0, keepdims=True), scale_two]
    for j in range(n):
        pmsg[j, 8:16, :] = jnp.zeros((8, 128), F32)
    for at in range(80):
        v, b = at // 4, at % 4
        pmsg[at // 3, 8 + at % 3 : 9 + at % 3, :] = lines[v][:, 128 * b : 128 * b + 128]
    prob_out, prob_back = part_to(pmsg, pgot, s_p1), part_from(pmine, pg_s, s_p2)
    start_all(prob_out)

    def grads(half, block, left, right):
        for side in range(2):
            g = dot(left[:, 256 * side : 256 * side + 256], right, 0, 0).astype(BF16)
            for r in range(4):
                at = 4 * side + r
                gl[half, at % 2, at // 2, :, 512 * block : 512 * block + 512] = g[
                    64 * r : 64 * r + 64
                ]

    def pair_copy(half, k):
        there = lax.rem(y + 1 + k, 4)
        return remote(
            gl.at[half, 1 - core, there],
            rb1.at[half, k],
            s_pair,
            4 * half + k,
            rep=2 * y + 1 - core,
        )

    def column_copy(half, k):
        there = lax.rem(y + 1 + k, 4)
        return remote(
            sb2.at[half, k], rb2.at[half, k], s_col, 3 * half + k, rep=2 * there + core
        )

    def pair_start(half):
        for k in range(4):
            pair_copy(half, k).start()

    def pair_finish(half):
        for k in range(3):
            there = lax.rem(y + 1 + k, 4)
            pair_copy(half, k).wait_recv()

            def add(i, k=k, there=there):
                at = ds(i * 16, 16)
                sb2[half, k, at, :] = (
                    gl[half, core, there, at, :].astype(F32) + rb1[half, k, at, :].astype(F32)
                ).astype(BF16)

            loop(4, add)
            column_copy(half, k).start()
        pair_copy(half, 3).wait_recv()

        def own(i):
            at = ds(i * 16, 16)
            acc2[half, at, :] = gl[half, core, y, at, :].astype(F32) + rb1[half, 3, at, :].astype(
                F32
            )

        loop(4, own)

    def third(half):
        def copy(k):
            j = lax.rem(me + k, n)
            return remote(sb3.at[half, j], rb3.at[half, k], s_third, n * half + k, sp=j)

        return copy

    def fourth(half):
        return lambda k: remote(
            fin.at[half], grads_ref.at[half, me], s_fourth, n * half + k, sp=lax.rem(me + k, n)
        )

    def column_finish(half):
        for k in range(3):
            column_copy(half, k).wait_recv()
        for j in range(n):
            rows, cols = chunk(j)
            total = acc2[half, rows, cols]
            for k in range(3):
                total = total + rb2[half, k, rows, cols].astype(F32)
            sb3[half, j] = total.astype(BF16)
        start_all(third(half))

    def third_finish(half):
        total = add_all(third(half), rb3.at[half], sb3[half, me].astype(F32)).astype(BF16)
        fin[half] = total
        grads_ref[half, me] = total
        start_all(fourth(half))

    for p in range(PAIRS):
        cols = slice(128 * p, 128 * p + 128)
        for i in range(0, TOK, 256):
            dmix_s[i : i + 256, 2 * D + 128 * p : 2 * D + 128 * p + 128] = dot(
                datt_s[i : i + 256, cols], bd_s[p], 1, 0
            ).astype(BF16)
    grads(1, 0, act1_s, dmix_s[:, 2 * D :])
    grads(1, 1, att_s, dproj_s[...])
    pair_start(1)
    total = add_all(prob_out, pgot, pmsg[me])
    pmine[...] = total[:8]
    start_all(prob_back)
    pg_s[me] = total[:8]
    ssend[...] = total[8:]

    def small_copy(k):
        return remote(ssend, srb.at[rep], s_small, k, rep=lax.rem(rep + k, reps))

    for k in range(1, reps):
        small_copy(k).start()
    srb[rep] = total[8:]
    pair_finish(1)
    received(prob_back)

    for p in range(PAIRS):
        prob, scores, divisor, sharp, query_norm, key_norm = pair_attention(
            p, gram_s, sq_s, sharp_ref, low, eye
        )
        pg = pg_s[8 * p : 8 * p + 8].reshape(HEAD_DIM, 128)
        logit = prob * (pg - half_sum(prob * pg, low))
        bd = block_diag(logit * sharp / divisor, low)
        weighted = logit * scores
        d_qsq = -half_sum(weighted, low) / (2.0 * query_norm * query_norm)
        d_qsq = jnp.sum(jnp.where(eye, d_qsq, 0.0), 0, keepdims=True)
        d_ksq = -jnp.sum(weighted, 0, keepdims=True) / (2.0 * key_norm * key_norm)
        qc = slice(128 * p, 128 * p + 128)
        kc = slice(D + 128 * p, D + 128 * p + 128)
        for i in range(0, TOK, 256):
            at = slice(i, i + 256)
            query, key = mixed_s[at, qc], mixed_s[at, kc]
            dmix_s[at, qc] = (dot(key, bd, 1, 1) + 2.0 * d_qsq * query.astype(F32)).astype(BF16)
            dmix_s[at, kc] = (dot(query, bd, 1, 0) + 2.0 * d_ksq * key.astype(F32)).astype(BF16)
    grads(0, 0, act1_s, dmix_s[:, :D])
    grads(0, 1, act1_s, dmix_s[:, D : 2 * D])
    pair_start(0)
    column_finish(1)
    pair_finish(0)

    def inputs(i):
        at = ds(i * 256, 256)
        dact_s[at, :] = dot(dmix_s[at, :], w_ref[...], 1, 1)

    loop(2, inputs)

    def input_rows(i):
        at = ds(i * 32, 32)
        normed, inverse = norm_parts(x_ref[at, :].astype(F32))
        lnb = norm_back(dact_s[at, :], gain1, normed, inverse)
        out_ref[at, :] = (dres_s[at, :] + lnb).astype(BF16)

    loop(TOK // 32, input_rows)
    column_finish(0)
    third_finish(1)
    for k in range(1, reps):
        small_copy(k).wait_recv()
    total = srb[0]
    for k in range(1, reps):
        total = total + srb[k]
    sfin[...] = total
    small_ref[me] = total
    fifth = part_from(sfin, small_ref, s_fifth)
    start_all(fifth)
    third_finish(0)

    for copy in (gram_out, gram_back, prob_out, prob_back, third(0), third(1)):
        sent(copy)
    for src, halo, sems in (
        (up_row[0], up_halo, s_up),
        (act_edge.at[0], act_halo, s_act),
        (dh_edge.at[0], dh_halo, s_dh),
    ):
        halos_sent(src, halo, sems)
    for k in range(1, reps):
        small_copy(k).wait_send()
    for half in range(2):
        for k in range(4):
            pair_copy(half, k).wait_send()
        for k in range(3):
            column_copy(half, k).wait_send()
    for copy in (fourth(1), fifth, fourth(0)):
        received(copy)
        sent(copy)


def finish(out_in, grads_ref, small_ref, out_ref, gq_ref, gp_ref, conv_ref, scale_ref):
    out_ref[...] = out_in[...]
    for j in range(32):
        rows, cols = chunk(j)
        gq_ref[rows, cols] = grads_ref[0, j].astype(F32)
        if cols.start < D:
            gq_ref[rows, 2 * D + cols.start : 2 * D + cols.stop] = grads_ref[1, j].astype(F32)
        else:
            gp_ref[rows, cols.start - D : cols.stop - D] = grads_ref[1, j].astype(F32)
    for at in range(80):
        v, b = at // 4, at % 4
        line = small_ref[at // 3, at % 3 : at % 3 + 1, :]
        lanes = slice(128 * b, 128 * b + 128)
        if v < 18:
            conv_ref[v // 9, (v // 3) % 3, v % 3 : v % 3 + 1, lanes] = line
        else:
            scale_ref[v - 18 : v - 17, lanes] = line


def call(body, name, outs, scratch, args, smem=0, collective=None):
    params = dict(vmem_limit_bytes=LIMIT)
    if collective is not None:
        params.update(collective_id=collective, has_side_effects=True)
    specs = [pl.BlockSpec(memory_space=pltpu.SMEM)] * smem
    specs += [pl.BlockSpec(memory_space=VMEM)] * (len(args) - smem)
    return pl.pallas_call(
        body,
        name=name,
        out_shape=[jax.ShapeDtypeStruct(s, t) for s, t in outs],
        in_specs=specs,
        out_specs=[pl.BlockSpec(memory_space=VMEM)] * len(outs),
        scratch_shapes=scratch,
        compiler_params=pltpu.CompilerParams(**params),
    )(*args)


def shards(n, x, up, gain1, w, sharp, wo, factors, gain2, kernels):
    x = x.reshape(TOK, D)
    up = up.reshape(TOK, D)
    gain1, gain2 = gain1.reshape(1, D), gain2.reshape(1, D)
    scratch = [
        VMEM((TOK, D), BF16),
        VMEM((TOK, 3 * D), BF16),
        VMEM((n, 16, 128), F32),
        VMEM((n, 16, 128), F32),
        VMEM((8, 128), F32),
        VMEM((n, 8, 128), F32),
        VMEM((8, 128), F32),
        VMEM((18, D), F32),
        VMEM((2, WIDTH, D), BF16),
        VMEM((2, WIDTH, D), BF16),
        VMEM((2, WIDTH, D), BF16),
        VMEM((2, WIDTH, D), BF16),
        VMEM((2, WIDTH, D), BF16),
        VMEM((4, 272, D), F32),
        VMEM((4, 272, D), F32),
        VMEM((4, 272, D), F32),
        VMEM((2, 272, D), F32),
        VMEM((TOK, D), F32),
        VMEM((PAIRS, 128, 128), BF16),
        VMEM((TOK, D), BF16),
        VMEM((TOK, D), F32),
        VMEM((TOK, D), F32),
        VMEM((TOK, 128), F32),
        VMEM((TOK, D), F32),
        VMEM((18, 8, D), F32),
        VMEM((TOK, D), BF16),
        VMEM((TOK, D), F32),
        VMEM((TOK, D), BF16),
        VMEM((TOK, 3 * D), BF16),
        VMEM((n, 16, 128), F32),
        VMEM((n, 16, 128), F32),
        VMEM((8, 128), F32),
        VMEM((n, 8, 128), F32),
        VMEM((2, 2, 4, 64, 1024), BF16),
        VMEM((2, 4, 64, 1024), BF16),
        VMEM((2, 3, 64, 1024), BF16),
        VMEM((2, 3, 64, 1024), BF16),
        VMEM((2, 64, 1024), F32),
        VMEM((2, n, 16, 128), BF16),
        VMEM((2, n, 16, 128), BF16),
        VMEM((2, 16, 128), BF16),
        VMEM((8, 8, 128), F32),
        VMEM((8, 128), F32),
        VMEM((8, 128), F32),
    ]
    for count in (n, n, n, n, 2, 2, 2, 8, 6, 2 * n, 2 * n, 8, n):
        scratch.append(pltpu.SemaphoreType.DMA((2, count)))
    out, grads, small = call(
        functools.partial(layer, n),
        "layer",
        [((TOK, D), BF16), ((2, n, 16, 128), BF16), ((n, 8, 128), F32)],
        scratch,
        (sharp, x, up, gain1, w, wo, factors, gain2, kernels),
        smem=1,
        collective=0,
    )
    out, gq, gp, conv, scale = call(
        finish,
        "finish",
        [
            ((TOK, D), BF16),
            ((64, 3 * D), F32),
            ((64, D), F32),
            ((2, 3, 3, D), F32),
            ((2, D), F32),
        ],
        [],
        (out, grads, small),
    )
    return out.reshape(1, 2, WIDTH, D), gq, gp, conv, scale


def solution(mesh):
    tokens = P("rep", "sp", None, None)
    in_specs = (tokens, tokens, P(), P(), P(), P(), P(), P(), P())
    out_specs = (tokens, P("rep", None), P("rep", None), P(), P())
    return jax.shard_map(
        functools.partial(shards, mesh.shape["sp"]),
        mesh=mesh,
        in_specs=in_specs,
        out_specs=out_specs,
        check_vma=False,
    )
```

time: 311 us -> 111 us (0.36)
  Pallas kernels: 0 us -> 106 us
  starting transfers between devices: 106 us -> 0 us
  waiting for transfers between devices: 69.9 us -> 0 us
  other arithmetic: 56.6 us -> 0 us
  local copies, waits for them, and re-layouts: 43.8 us -> 2.84 us
  matrix products: 18.4 us -> 0 us
  blocking collectives: 10.4 us -> 0 us
    pallas_call x0 -> x2, Pallas kernels: none -> 106 us  [call(): pl.pallas_call(body, name=name, out_shape=[jax.ShapeDtypeStruct(s, t) for...]
    all_to_all x11 -> x0, starting transfers between devices: 84.1 us -> none  [the longest x4 42.9 us: sum_at_owner(): lax.all_to_all(tiles, axis, split_axis=0, concat_axis=0, tiled=True)]
    all_to_all x11 -> x0, waiting for transfers between devices: 65.9 us -> none  [the longest x2 27.4 us: sum_by_axis(): return jnp.sum(lax.all_to_all(own, far, 0, 0, tiled=True), axis=0)]
    reduce_sum x20 -> x0, other arithmetic: 27.5 us -> none  [the longest x5 6.2 us: sum_at_owner(): return arrived.sum(axis=0)]
    ppermute x8 -> x0, starting transfers between devices: 21.7 us -> none  [the longest x4 12.3 us: shifted_2(): lax.ppermute(value, axis, [(source, source + steps) for source in range(l...]
    dot_general x12 -> x0, matrix products: 18.4 us -> none  [the longest x1 2.67 us: shards(): lax.dot_general(d_mixed, triple_mapping_matrix, (((1,), (1,)), ((), ())),...]
    slice x23 -> x0, local copies, waits for them, and re-layouts: 17.6 us -> none  [the longest x5 5.59 us: packed_total(): total[b:e].reshape(a.shape)]
    all_to_all x1 -> x0, blocking collectives: 10.4 us -> none  [sum_at_owner(): lax.all_to_all(tiles, axis, split_axis=0, concat_axis=0, tiled=True)]
  transfers between devices with their start and end apart: 19 -> 0, of which waited for: 10 -> 0; matrix products, arithmetic and copies ran while one was open for 26% -> 0% of each run, Pallas kernels for 0% -> 0%
where the time goes in v2:
time: 111 us; the launch traced here: 110 us
  Pallas kernels  106 us (95%)
  local copies, waits for them, and re-layouts  2.84 us (3%)
    pallas_call x2, Pallas kernels, call(): pl.pallas_call(body, name=name, out_shape=[jax.ShapeDtypeStruct(s, t) for...  106 us
    unnamed x2, local copies, waits for them, and re-layouts  2.84 us

profile of v2, /device:TPU:1, one launch (start us, length us, event | category | flops | bytes accessed | tf_op | source)
XLA Modules:
  0.0 109.9 jit_solution(10117608285322401089)
XLA Ops:
  0.6 1.4 %copy.14.kern4_ref = f32[2,3,3,512]{3,2,1,0:T(4,128)} copy(f32[2,3,3,512]{3,0,2,1:T(2,128)} %param.17) | data formatting | bytes 73728 | tf_op args[8]
  2.0 104.2 %layer.1 = (bf16[512,512]{1,0:T(8,128)(2,1)}, bf16[2,32,16,128]{3,2,1,0:T(8,128)(2,1)}, f32[32,8,128]{2,1,0:T(8,128)}) custom-call(f32[8]{0:T(128)} %sharp_ref.1, bf16[512,512]{1,0:T(8,128)(2,1)} %bitcast.5, bf16[512,512]{1,0:T(8,128)(2,1)} %bitcast.6, f32[1,512]{1,0:T(1,128)} %bitcast.7, bf16[512,1536]{1,0:T(8,128)(2,1)} %w_ref.1, bf16[512,512]{1,0:T(8,128)(2,1)} %wo_ref.1, ...), custom_call_target="tpu_custom_call" | custom-call | tf_op jit(solution)/shard_map/layer/pallas_call | solution.py:681
  106.3 2.2 %finish.1 = (bf16[512,512]{1,0:T(8,128)(2,1)}, f32[64,1536]{1,0:T(8,128)}, f32[64,512]{1,0:T(8,128)}, f32[2,3,3,512]{3,2,1,0:T(4,128)}, f32[2,512]{1,0:T(2,128)}) custom-call(bf16[512,512]{1,0:T(8,128)(2,1)} %get-tuple-element.13.out_in, bf16[2,32,16,128]{3,2,1,0:T(8,128)(2,1)} %get-tuple-element.14.grads_ref, f32[32,8,128]{2,1,0:T(8,128)} %get-tuple-element.15.small_ref), custom_call_target="tpu_custom_call" | custom-call | tf_op jit(solution)/shard_map/finish/pallas_call | solution.py:681
  108.4 1.4 %copy.15 = f32[2,3,3,512]{3,0,2,1:T(2,128)} copy(f32[2,3,3,512]{3,2,1,0:T(4,128)} %get-tuple-element.24) | data formatting | bytes 73728

commit v3 on v2

--- a/solution.py
+++ b/solution.py
@@ -101,12 +101,13 @@
     )
 
 
-def loop(count, step, first=0):
+def loop(count, step, first=0, each=1):
     def go(i, _):
-        step(i)
+        for u in range(each):
+            step(i * each + u)
         return 0
 
-    lax.fori_loop(first, count, go, 0)
+    lax.fori_loop(first, count // each, go, 0)
 
 
 def fold(v):
@@ -121,22 +122,29 @@
     n,
     sharp_ref,
     x_ref,
-    up_ref,
+    up_hbm,
     gain1_ref,
-    w_ref,
-    wo_ref,
+    w_hbm,
+    wo_hbm,
     factor_ref,
     gain2_ref,
     kern4_ref,
     out_ref,
     grads_ref,
     small_ref,
+    up_ref,
+    w_ref,
+    wo_ref,
     act1_s,
     mixed_s,
     gmsg,
     ggot,
     gmine,
     gram_s,
+    gsq,
+    gsqgot,
+    gsqmine,
+    sq_all,
     sq_s,
     kern_ref,
     up_halo,
@@ -150,6 +158,7 @@
     hid_s,
     dhid_s,
     bd_s,
+    bd2_s,
     att_s,
     proj_s,
     normed_s,
@@ -164,6 +173,15 @@
     pgot,
     pmine,
     pg_s,
+    smsg,
+    sgot,
+    pm_s,
+    actp_s,
+    mbuf,
+    mgot,
+    mtot,
+    qs,
+    qgot,
     gl,
     rb1,
     sb2,
@@ -175,13 +193,19 @@
     srb,
     ssend,
     sfin,
+    s_load,
     s_g1,
     s_g2,
+    s_q1,
+    s_q2,
     s_p1,
     s_p2,
+    s_s1,
     s_up,
     s_act,
     s_dh,
+    s_m,
+    s_qx,
     s_pair,
     s_col,
     s_third,
@@ -191,6 +215,12 @@
 ):
     me, rep = lax.axis_index("sp"), lax.axis_index("rep")
     reps = 8
+    loads = [
+        pltpu.make_async_copy(src, dst, s_load.at[0, at])
+        for at, (src, dst) in enumerate(((w_hbm, w_ref), (up_hbm, up_ref), (wo_hbm, wo_ref)))
+    ]
+    for load in loads:
+        load.start()
     y, core = rep // 2, lax.rem(rep, 2)
     barrier = pltpu.get_barrier_semaphore()
 
@@ -267,8 +297,12 @@
     def part_from(mine, total, sems):
         return lambda k: remote(mine, total.at[me], sems, k, sp=lax.rem(me + k, n))
 
-    def start_all(copy):
-        loop(n, lambda k: copy(k).start(), 1)
+    def start_all(*copies):
+        def start(k):
+            for copy in copies:
+                copy(k).start()
+
+        loop(n, start, 1)
 
     def add_all(copy, got, own):
         def add(k, total):
@@ -288,7 +322,8 @@
         normed, _ = norm_parts(x_ref[at, :].astype(F32))
         act1_s[at, :] = (normed * gain1).astype(BF16)
 
-    loop(TOK // 32, norm_one)
+    loop(TOK // 32, norm_one, each=4)
+    loads[0].wait()
 
     def mix(i):
         at = ds(i * 256, 256)
@@ -308,18 +343,43 @@
         key = mixed_s[:, D + 128 * p : D + 128 * p + 128]
         packed = pack_pair(dot(query, key, 0, 0), low)
         for b in range(8):
-            gmsg[8 * p + b, 0:8, :] = packed[8 * b : 8 * b + 8]
+            gmsg[8 * p + b] = packed[8 * b : 8 * b + 8]
+    quarter = lax.broadcasted_iota(jnp.int32, (1, 128), 1) >> 5
     for j in range(n):
-        gmsg[j, 8:16, :] = sq
+        gsq[j] = jnp.where(quarter == j % 4, sq[j // 4 : j // 4 + 1], 0.0)
     pl.semaphore_wait(barrier, n - 1 + reps - 1)
     gram_out, gram_back = part_to(gmsg, ggot, s_g1), part_from(gmine, gram_s, s_g2)
-    start_all(gram_out)
+    sq_out, sq_back = part_to(gsq, gsqgot, s_q1), part_from(gsqmine, sq_all, s_q2)
+    start_all(gram_out, sq_out)
     up_row = [up_ref.at[pl.ds(0, WIDTH)], up_ref.at[pl.ds(WIDTH, WIDTH)]]
-    send_above(up_row[0], up_halo, s_up)
-    send_below(up_row[1], up_halo, s_up)
+
+    def product_copy(p):
+        def copy(k):
+            j = lax.rem(me + k, n)
+            return remote(mbuf.at[p, j], mgot.at[p, k], s_m, n * p + k, sp=j)
+
+        return copy
+
+    def product(p):
+        for at in range(2):
+            cols = slice(512 * at + 128 * p, 512 * at + 128 * p + 128)
+            part = dot(actp_s[...], mixed_s[:, cols], 0, 0).astype(BF16)
+            mbuf[p, :, :, 128 * at : 128 * at + 128] = part.reshape(n, 16, 128)
+
+    lane = lax.broadcasted_iota(jnp.int32, (64, D), 1)
+    line = lax.broadcasted_iota(jnp.int32, (64, D), 0)
+    spot = (line >> 1) * 16 + (line & 1)
+    for r in range(8):
+        pm_s[64 * r : 64 * r + 64, :] = jnp.where(lane == spot + 2 * r, 1.0, 0.0).astype(BF16)
+    for i in range(0, TOK, 256):
+        actp_s[i : i + 256, :] = dot(act1_s[i : i + 256, :], pm_s[...], 1, 0).astype(BF16)
+    product(0)
+    start_all(product_copy(0))
+    for p in range(1, PAIRS):
+        product(p)
 
     for at in range(18):
-        kern_ref[at : at + 1, :] = kern4_ref[at // 9, (at // 3) % 3, at % 3 : at % 3 + 1, :]
+        kern_ref[at : at + 1, :] = kern4_ref[(at // 3) % 3, at % 3, at // 9 : at // 9 + 1, :]
     for ref, count in ((act_s, 4), (up_s, 4), (dh_s, 4), (hid_s, 2)):
         for r in range(count):
             ref[r, 0:8, :] = jnp.zeros((8, D), F32)
@@ -330,13 +390,24 @@
         row, c = i // 4, lax.rem(i, 4)
         up_s[row + 1, ds(8 + c * 64, 64, 8), :] = up_ref[ds(i * 64, 64), :].astype(F32)
 
+    loads[1].wait()
     loop(8, upstream_rows)
     total = add_all(gram_out, ggot, gmsg[me])
-    gmine[...] = total[:8]
-    start_all(gram_back)
-    gram_s[me] = total[:8]
-    sq_s[...] = total[8:]
+    gmine[...] = total
+    gram_s[me] = total
+    total = add_all(sq_out, gsqgot, gsq[me])
+    gsqmine[...] = total
+    sq_all[me] = total
+    start_all(gram_back, sq_back)
+    send_above(up_row[0], up_halo, s_up)
+    send_below(up_row[1], up_halo, s_up)
+    start_all(product_copy(1))
+    start_all(product_copy(3))
+    loads[2].wait()
     received(gram_back)
+    received(sq_back)
+    for p in range(2 * PAIRS):
+        sq_s[p : p + 1, :] = sq_all[4 * p] + sq_all[4 * p + 1] + sq_all[4 * p + 2] + sq_all[4 * p + 3]
 
     for p in range(PAIRS):
         prob = pair_attention(p, gram_s, sq_s, sharp_ref, low, eye)[0]
@@ -359,7 +430,7 @@
             normed_s[at, :] = normed
             inv_s[at, :] = jnp.broadcast_to(inverse, (32, 128))
 
-        loop(WIDTH // 32, norm_two)
+        loop(WIDTH // 32, norm_two, each=4)
         if row == 0:
             send_above(act_edge.at[0], act_halo, s_act)
         else:
@@ -412,6 +483,7 @@
             send_above(dh_edge.at[0], dh_halo, s_dh)
         else:
             send_below(dh_edge.at[1], dh_halo, s_dh)
+    start_all(product_copy(2))
 
     def kernel_grads(idx):
         r = idx // 16
@@ -444,16 +516,19 @@
 
     loop(32, act_grads)
 
-    def residual_rows(i, scale):
-        row, c = i // 8, lax.rem(i, 8)
-        at = ds(i * 32, 32)
-        lnb = norm_back(dact_s[at, :], gain2, normed_s[at, :], inv_s[at, 0:1])
-        d_res = up_s[row + 1, ds(8 + c * 32, 32, 8), :] + lnb
-        dres_s[at, :] = d_res
-        dproj_s[at, :] = (factor0 * d_res).astype(BF16)
-        return scale + fold(proj_s[at, :] * d_res)
-
-    scale_one = lax.fori_loop(0, TOK // 32, residual_rows, jnp.zeros((8, D), F32))
+    def residual_rows(step, scale):
+        for u in range(4):
+            i = 4 * step + u
+            row, c = i // 8, lax.rem(i, 8)
+            at = ds(i * 32, 32)
+            lnb = norm_back(dact_s[at, :], gain2, normed_s[at, :], inv_s[at, 0:1])
+            d_res = up_s[row + 1, ds(8 + c * 32, 32, 8), :] + lnb
+            dres_s[at, :] = d_res
+            dproj_s[at, :] = (factor0 * d_res).astype(BF16)
+            scale = scale + fold(proj_s[at, :] * d_res)
+        return scale
+
+    scale_one = lax.fori_loop(0, TOK // 128, residual_rows, jnp.zeros((8, D), F32))
 
     def attended_rows(i):
         at = ds(i * 256, 256)
@@ -465,98 +540,79 @@
         value = mixed_s[:, 2 * D + 128 * p : 2 * D + 128 * p + 128]
         packed = pack_pair(dot(datt_s[:, cols], value, 0, 0), low)
         for b in range(8):
-            pmsg[8 * p + b, 0:8, :] = packed[8 * b : 8 * b + 8]
+            pmsg[8 * p + b] = packed[8 * b : 8 * b + 8]
+    prob_out, prob_back = part_to(pmsg, pgot, s_p1), part_from(pmine, pg_s, s_p2)
+    start_all(prob_out)
     lines = [acc_s[m].sum(0, keepdims=True) for m in range(18)]
     scale_two = sum(lines[9 + m] * kern_ref[9 + m : 10 + m, :] for m in range(9))
     lines = lines[:9] + [line * factor1 for line in lines[9:]]
     lines += [scale_one.sum(0, keepdims=True), scale_two]
-    for j in range(n):
-        pmsg[j, 8:16, :] = jnp.zeros((8, 128), F32)
+    smsg[...] = jnp.zeros_like(smsg)
     for at in range(80):
         v, b = at // 4, at % 4
-        pmsg[at // 3, 8 + at % 3 : 9 + at % 3, :] = lines[v][:, 128 * b : 128 * b + 128]
-    prob_out, prob_back = part_to(pmsg, pgot, s_p1), part_from(pmine, pg_s, s_p2)
-    start_all(prob_out)
-
-    def grads(half, block, left, right):
+        smsg[at // 3, at % 3 : at % 3 + 1, :] = lines[v][:, 128 * b : 128 * b + 128]
+    small_out = part_to(smsg, sgot, s_s1)
+    start_all(small_out)
+
+    def grads(block, left, right):
         for side in range(2):
             g = dot(left[:, 256 * side : 256 * side + 256], right, 0, 0).astype(BF16)
             for r in range(4):
                 at = 4 * side + r
-                gl[half, at % 2, at // 2, :, 512 * block : 512 * block + 512] = g[
-                    64 * r : 64 * r + 64
-                ]
-
-    def pair_copy(half, k):
+                gl[at % 2, at // 2, :, 512 * block : 512 * block + 512] = g[64 * r : 64 * r + 64]
+
+    def pair_copy(k):
         there = lax.rem(y + 1 + k, 4)
-        return remote(
-            gl.at[half, 1 - core, there],
-            rb1.at[half, k],
-            s_pair,
-            4 * half + k,
-            rep=2 * y + 1 - core,
-        )
-
-    def column_copy(half, k):
+        return remote(gl.at[1 - core, there], rb1.at[k], s_pair, k, rep=2 * y + 1 - core)
+
+    def column_copy(k):
         there = lax.rem(y + 1 + k, 4)
-        return remote(
-            sb2.at[half, k], rb2.at[half, k], s_col, 3 * half + k, rep=2 * there + core
-        )
-
-    def pair_start(half):
-        for k in range(4):
-            pair_copy(half, k).start()
-
-    def pair_finish(half):
+        return remote(sb2.at[k], rb2.at[k], s_col, k, rep=2 * there + core)
+
+    def pair_finish():
         for k in range(3):
             there = lax.rem(y + 1 + k, 4)
-            pair_copy(half, k).wait_recv()
+            pair_copy(k).wait_recv()
 
             def add(i, k=k, there=there):
                 at = ds(i * 16, 16)
-                sb2[half, k, at, :] = (
-                    gl[half, core, there, at, :].astype(F32) + rb1[half, k, at, :].astype(F32)
+                sb2[k, at, :] = (
+                    gl[core, there, at, :].astype(F32) + rb1[k, at, :].astype(F32)
                 ).astype(BF16)
 
             loop(4, add)
-            column_copy(half, k).start()
-        pair_copy(half, 3).wait_recv()
+            column_copy(k).start()
+        pair_copy(3).wait_recv()
 
         def own(i):
             at = ds(i * 16, 16)
-            acc2[half, at, :] = gl[half, core, y, at, :].astype(F32) + rb1[half, 3, at, :].astype(
-                F32
-            )
+            acc2[at, :] = gl[core, y, at, :].astype(F32) + rb1[3, at, :].astype(F32)
 
         loop(4, own)
 
-    def third(half):
-        def copy(k):
-            j = lax.rem(me + k, n)
-            return remote(sb3.at[half, j], rb3.at[half, k], s_third, n * half + k, sp=j)
-
-        return copy
+    def third(k):
+        j = lax.rem(me + k, n)
+        return remote(sb3.at[j], rb3.at[k], s_third, k, sp=j)
 
     def fourth(half):
         return lambda k: remote(
             fin.at[half], grads_ref.at[half, me], s_fourth, n * half + k, sp=lax.rem(me + k, n)
         )
 
-    def column_finish(half):
+    def column_finish():
         for k in range(3):
-            column_copy(half, k).wait_recv()
+            column_copy(k).wait_recv()
         for j in range(n):
             rows, cols = chunk(j)
-            total = acc2[half, rows, cols]
+            total = acc2[rows, cols]
             for k in range(3):
-                total = total + rb2[half, k, rows, cols].astype(F32)
-            sb3[half, j] = total.astype(BF16)
-        start_all(third(half))
-
-    def third_finish(half):
-        total = add_all(third(half), rb3.at[half], sb3[half, me].astype(F32)).astype(BF16)
-        fin[half] = total
-        grads_ref[half, me] = total
+                total = total + rb2[k, rows, cols].astype(F32)
+            sb3[j] = total.astype(BF16)
+        start_all(third)
+
+    def to_everyone(half, total):
+        fin[half] = total.astype(BF16)
+        grads_ref[half, me] = total.astype(BF16)
         start_all(fourth(half))
 
     for p in range(PAIRS):
@@ -565,63 +621,85 @@
             dmix_s[i : i + 256, 2 * D + 128 * p : 2 * D + 128 * p + 128] = dot(
                 datt_s[i : i + 256, cols], bd_s[p], 1, 0
             ).astype(BF16)
-    grads(1, 0, act1_s, dmix_s[:, 2 * D :])
-    grads(1, 1, att_s, dproj_s[...])
-    pair_start(1)
+    grads(0, act1_s, dmix_s[:, 2 * D :])
+    grads(1, att_s, dproj_s[...])
+    for k in range(4):
+        pair_copy(k).start()
+    for p in range(PAIRS):
+        total = add_all(product_copy(p), mgot.at[p], mbuf[p, me].astype(F32))
+        mtot[:, 128 * p : 128 * p + 128] = total[:, :128]
+        mtot[:, D + 128 * p : D + 128 * p + 128] = total[:, 128:]
+    pair_finish()
     total = add_all(prob_out, pgot, pmsg[me])
-    pmine[...] = total[:8]
+    pmine[...] = total
     start_all(prob_back)
-    pg_s[me] = total[:8]
-    ssend[...] = total[8:]
+    pg_s[me] = total
+    total = add_all(small_out, sgot, smsg[me])
+    ssend[...] = total
+    srb[rep] = total
 
     def small_copy(k):
         return remote(ssend, srb.at[rep], s_small, k, rep=lax.rem(rep + k, reps))
 
     for k in range(1, reps):
         small_copy(k).start()
-    srb[rep] = total[8:]
-    pair_finish(1)
+    column_finish()
     received(prob_back)
 
+    def split_dot(a, b, ca, cb):
+        high = a.astype(BF16)
+        rest = (a - high.astype(F32)).astype(BF16)
+        return dot(high, b, ca, cb) + dot(rest, b, ca, cb)
+
+    squares = []
     for p in range(PAIRS):
         prob, scores, divisor, sharp, query_norm, key_norm = pair_attention(
             p, gram_s, sq_s, sharp_ref, low, eye
         )
         pg = pg_s[8 * p : 8 * p + 8].reshape(HEAD_DIM, 128)
         logit = prob * (pg - half_sum(prob * pg, low))
-        bd = block_diag(logit * sharp / divisor, low)
+        bd2_s[p] = block_diag(logit * sharp / divisor, low)
         weighted = logit * scores
         d_qsq = -half_sum(weighted, low) / (2.0 * query_norm * query_norm)
-        d_qsq = jnp.sum(jnp.where(eye, d_qsq, 0.0), 0, keepdims=True)
-        d_ksq = -jnp.sum(weighted, 0, keepdims=True) / (2.0 * key_norm * key_norm)
+        d_qsq = 2.0 * jnp.sum(jnp.where(eye, d_qsq, 0.0), 0, keepdims=True)
+        d_ksq = -2.0 * jnp.sum(weighted, 0, keepdims=True) / (2.0 * key_norm * key_norm)
+        squares.append((d_qsq, d_ksq))
+        by_query = mtot[:, 128 * p : 128 * p + 128]
+        by_key = mtot[:, D + 128 * p : D + 128 * p + 128]
+        g_query = split_dot(by_key, bd2_s[p], 1, 1) + d_qsq * by_query
+        g_key = split_dot(by_query, bd2_s[p], 1, 0) + d_ksq * by_key
+        for r in range(reps):
+            qs[r, 2 * p : 2 * p + 2, :] = g_query[2 * r : 2 * r + 2]
+            qs[r, 8 + 2 * p : 10 + 2 * p, :] = g_key[2 * r : 2 * r + 2]
+
+    def query_copy(k):
+        there = lax.rem(rep + k, reps)
+        return remote(qs.at[there], qgot.at[rep], s_qx, k, rep=there)
+
+    for k in range(1, reps):
+        query_copy(k).start()
+    qgot[rep] = qs[rep]
+    for p in range(PAIRS):
+        d_qsq, d_ksq = squares[p]
         qc = slice(128 * p, 128 * p + 128)
         kc = slice(D + 128 * p, D + 128 * p + 128)
         for i in range(0, TOK, 256):
             at = slice(i, i + 256)
             query, key = mixed_s[at, qc], mixed_s[at, kc]
-            dmix_s[at, qc] = (dot(key, bd, 1, 1) + 2.0 * d_qsq * query.astype(F32)).astype(BF16)
-            dmix_s[at, kc] = (dot(query, bd, 1, 0) + 2.0 * d_ksq * key.astype(F32)).astype(BF16)
-    grads(0, 0, act1_s, dmix_s[:, :D])
-    grads(0, 1, act1_s, dmix_s[:, D : 2 * D])
-    pair_start(0)
-    column_finish(1)
-    pair_finish(0)
+            dmix_s[at, qc] = (dot(key, bd2_s[p], 1, 1) + d_qsq * query.astype(F32)).astype(BF16)
+            dmix_s[at, kc] = (dot(query, bd2_s[p], 1, 0) + d_ksq * key.astype(F32)).astype(BF16)
 
     def inputs(i):
         at = ds(i * 256, 256)
         dact_s[at, :] = dot(dmix_s[at, :], w_ref[...], 1, 1)
 
     loop(2, inputs)
-
-    def input_rows(i):
-        at = ds(i * 32, 32)
-        normed, inverse = norm_parts(x_ref[at, :].astype(F32))
-        lnb = norm_back(dact_s[at, :], gain1, normed, inverse)
-        out_ref[at, :] = (dres_s[at, :] + lnb).astype(BF16)
-
-    loop(TOK // 32, input_rows)
-    column_finish(0)
-    third_finish(1)
+    for k in range(1, reps):
+        query_copy(k).wait_recv()
+    total = qgot[0]
+    for k in range(1, reps):
+        total = total + qgot[k]
+    to_everyone(0, total)
     for k in range(1, reps):
         small_copy(k).wait_recv()
     total = srb[0]
@@ -631,10 +709,20 @@
     small_ref[me] = total
     fifth = part_from(sfin, small_ref, s_fifth)
     start_all(fifth)
-    third_finish(0)
-
-    for copy in (gram_out, gram_back, prob_out, prob_back, third(0), third(1)):
+    to_everyone(1, add_all(third, rb3, sb3[me].astype(F32)))
+
+    def input_rows(i):
+        at = ds(i * 32, 32)
+        normed, inverse = norm_parts(x_ref[at, :].astype(F32))
+        lnb = norm_back(dact_s[at, :], gain1, normed, inverse)
+        out_ref[at, :] = (dres_s[at, :] + lnb).astype(BF16)
+
+    loop(TOK // 32, input_rows, each=4)
+
+    for copy in (gram_out, gram_back, sq_out, sq_back, prob_out, prob_back, small_out, third):
         sent(copy)
+    for p in range(PAIRS):
+        sent(product_copy(p))
     for src, halo, sems in (
         (up_row[0], up_halo, s_up),
         (act_edge.at[0], act_halo, s_act),
@@ -643,12 +731,12 @@
         halos_sent(src, halo, sems)
     for k in range(1, reps):
         small_copy(k).wait_send()
-    for half in range(2):
-        for k in range(4):
-            pair_copy(half, k).wait_send()
-        for k in range(3):
-            column_copy(half, k).wait_send()
-    for copy in (fourth(1), fifth, fourth(0)):
+        query_copy(k).wait_send()
+    for k in range(4):
+        pair_copy(k).wait_send()
+    for k in range(3):
+        column_copy(k).wait_send()
+    for copy in (fourth(0), fifth, fourth(1)):
         received(copy)
         sent(copy)
 
@@ -657,7 +745,9 @@
     out_ref[...] = out_in[...]
     for j in range(32):
         rows, cols = chunk(j)
-        gq_ref[rows, cols] = grads_ref[0, j].astype(F32)
+        own = grads_ref[0, j].astype(F32)
+        for q in range(8):
+            gq_ref[2 * j : 2 * j + 2, 128 * q : 128 * q + 128] = own[2 * q : 2 * q + 2]
         if cols.start < D:
             gq_ref[rows, 2 * D + cols.start : 2 * D + cols.stop] = grads_ref[1, j].astype(F32)
         else:
@@ -667,17 +757,19 @@
         line = small_ref[at // 3, at % 3 : at % 3 + 1, :]
         lanes = slice(128 * b, 128 * b + 128)
         if v < 18:
-            conv_ref[v // 9, (v // 3) % 3, v % 3 : v % 3 + 1, lanes] = line
+            conv_ref[(v // 3) % 3, v % 3, v // 9 : v // 9 + 1, lanes] = line
         else:
             scale_ref[v - 18 : v - 17, lanes] = line
 
 
-def call(body, name, outs, scratch, args, smem=0, collective=None):
+def call(body, name, outs, scratch, args, smem=0, collective=None, away=()):
     params = dict(vmem_limit_bytes=LIMIT)
     if collective is not None:
         params.update(collective_id=collective, has_side_effects=True)
     specs = [pl.BlockSpec(memory_space=pltpu.SMEM)] * smem
-    specs += [pl.BlockSpec(memory_space=VMEM)] * (len(args) - smem)
+    specs += [
+        pl.BlockSpec(memory_space=pl.ANY if at in away else VMEM) for at in range(smem, len(args))
+    ]
     return pl.pallas_call(
         body,
         name=name,
@@ -693,53 +785,36 @@
     x = x.reshape(TOK, D)
     up = up.reshape(TOK, D)
     gain1, gain2 = gain1.reshape(1, D), gain2.reshape(1, D)
-    scratch = [
-        VMEM((TOK, D), BF16),
-        VMEM((TOK, 3 * D), BF16),
-        VMEM((n, 16, 128), F32),
-        VMEM((n, 16, 128), F32),
-        VMEM((8, 128), F32),
-        VMEM((n, 8, 128), F32),
-        VMEM((8, 128), F32),
-        VMEM((18, D), F32),
-        VMEM((2, WIDTH, D), BF16),
-        VMEM((2, WIDTH, D), BF16),
-        VMEM((2, WIDTH, D), BF16),
-        VMEM((2, WIDTH, D), BF16),
-        VMEM((2, WIDTH, D), BF16),
-        VMEM((4, 272, D), F32),
-        VMEM((4, 272, D), F32),
-        VMEM((4, 272, D), F32),
-        VMEM((2, 272, D), F32),
-        VMEM((TOK, D), F32),
-        VMEM((PAIRS, 128, 128), BF16),
-        VMEM((TOK, D), BF16),
-        VMEM((TOK, D), F32),
-        VMEM((TOK, D), F32),
-        VMEM((TOK, 128), F32),
-        VMEM((TOK, D), F32),
-        VMEM((18, 8, D), F32),
-        VMEM((TOK, D), BF16),
-        VMEM((TOK, D), F32),
-        VMEM((TOK, D), BF16),
-        VMEM((TOK, 3 * D), BF16),
-        VMEM((n, 16, 128), F32),
-        VMEM((n, 16, 128), F32),
-        VMEM((8, 128), F32),
-        VMEM((n, 8, 128), F32),
-        VMEM((2, 2, 4, 64, 1024), BF16),
+    kernels = kernels.transpose(1, 2, 0, 3)
+    row = VMEM((n, 8, 128), F32)
+    edge = VMEM((2, WIDTH, D), BF16)
+    wide, tall = VMEM((TOK, D), BF16), VMEM((TOK, D), F32)
+    scratch = [wide, VMEM((D, 3 * D), BF16), wide, wide, VMEM((TOK, 3 * D), BF16)]
+    scratch += [row, row, VMEM((8, 128), F32), row]
+    scratch += [VMEM((n, 1, 128), F32), VMEM((n, 1, 128), F32), VMEM((1, 128), F32)]
+    scratch += [VMEM((n, 1, 128), F32), VMEM((8, 128), F32), VMEM((18, D), F32)]
+    scratch += [edge] * 5
+    scratch += [VMEM((count, 272, D), F32) for count in (4, 4, 4, 2)]
+    scratch += [tall, VMEM((PAIRS, 128, 128), BF16), VMEM((PAIRS, 128, 128), BF16)]
+    scratch += [wide, tall, tall, VMEM((TOK, 128), F32), tall, VMEM((18, 8, D), F32)]
+    scratch += [wide, tall, wide, VMEM((TOK, 3 * D), BF16)]
+    scratch += [row, row, VMEM((8, 128), F32), row, row, row]
+    scratch += [wide, wide, VMEM((PAIRS, n, 16, 256), BF16), VMEM((PAIRS, n, 16, 256), BF16)]
+    scratch += [VMEM((16, 1024), F32), VMEM((8, 16, 128), F32), VMEM((8, 16, 128), F32)]
+    scratch += [
         VMEM((2, 4, 64, 1024), BF16),
-        VMEM((2, 3, 64, 1024), BF16),
-        VMEM((2, 3, 64, 1024), BF16),
-        VMEM((2, 64, 1024), F32),
-        VMEM((2, n, 16, 128), BF16),
-        VMEM((2, n, 16, 128), BF16),
+        VMEM((4, 64, 1024), BF16),
+        VMEM((3, 64, 1024), BF16),
+        VMEM((3, 64, 1024), BF16),
+        VMEM((64, 1024), F32),
+        VMEM((n, 16, 128), BF16),
+        VMEM((n, 16, 128), BF16),
         VMEM((2, 16, 128), BF16),
         VMEM((8, 8, 128), F32),
         VMEM((8, 128), F32),
         VMEM((8, 128), F32),
     ]
-    for count in (n, n, n, n, 2, 2, 2, 8, 6, 2 * n, 2 * n, 8, n):
+    for count in (3, n, n, n, n, n, n, n, 2, 2, 2, PAIRS * n, 8, 4, 3, n, 2 * n, 8, n):
         scratch.append(pltpu.SemaphoreType.DMA((2, count)))
     out, grads, small = call(
         functools.partial(layer, n),
@@ -749,6 +824,7 @@
         (sharp, x, up, gain1, w, wo, factors, gain2, kernels),
         smem=1,
         collective=0,
+        away=(2, 4, 5),
     )
     out, gq, gp, conv, scale = call(
         finish,
@@ -757,13 +833,13 @@
             ((TOK, D), BF16),
             ((64, 3 * D), F32),
             ((64, D), F32),
-            ((2, 3, 3, D), F32),
+            ((3, 3, 2, D), F32),
             ((2, D), F32),
         ],
         [],
         (out, grads, small),
     )
-    return out.reshape(1, 2, WIDTH, D), gq, gp, conv, scale
+    return out.reshape(1, 2, WIDTH, D), gq, gp, conv.transpose(2, 0, 1, 3), scale
 
 
 def solution(mesh):

time: 111 us -> 112 us (level)
  Pallas kernels: 106 us -> 111 us
  local copies, waits for them, and re-layouts: 2.84 us -> 0 us
    pallas_call x2, Pallas kernels: 106 us -> 111 us  [call(): pl.pallas_call(body, name=name, out_shape=[jax.ShapeDtypeStruct(s, t) for...]
    unnamed x2 -> x0, local copies, waits for them, and re-layouts: 2.84 us -> none
where the time goes in v3:
time: 112 us
  Pallas kernels  111 us (99%)
    pallas_call x2, Pallas kernels, call(): pl.pallas_call(body, name=name, out_shape=[jax.ShapeDtypeStruct(s, t) for...  111 us

profile of v3, /device:TPU:1, one launch (start us, length us, event | category | flops | bytes accessed | tf_op | source)
XLA Modules:
  0.0 112.0 jit_solution(5651419312200259349)
XLA Ops:
  0.6 109.1 %layer.1 = (bf16[512,512]{1,0:T(8,128)(2,1)}, bf16[2,32,16,128]{3,2,1,0:T(8,128)(2,1)}, f32[32,8,128]{2,1,0:T(8,128)}) custom-call(f32[8]{0:T(128)} %sharp_ref.1, bf16[512,512]{1,0:T(8,128)(2,1)} %bitcast.7, bf16[512,512]{1,0:T(8,128)(2,1)} %bitcast.8, f32[1,512]{1,0:T(1,128)} %bitcast.10, bf16[512,1536]{1,0:T(8,128)(2,1)} %w_hbm.1, ...), custom_call_target="tpu_custom_call" | custom-call | tf_op jit(solution)/shard_map/layer/pallas_call | solution.py:773
  109.8 2.2 %finish.1 = (bf16[512,512]{1,0:T(8,128)(2,1)}, f32[64,1536]{1,0:T(8,128)}, f32[64,512]{1,0:T(8,128)}, f32[3,3,2,512]{3,2,1,0:T(2,128)}, f32[2,512]{1,0:T(2,128)}) custom-call(bf16[512,512]{1,0:T(8,128)(2,1)} %get-tuple-element.13.out_in, bf16[2,32,16,128]{3,2,1,0:T(8,128)(2,1)} %get-tuple-element.14.grads_ref, f32[32,8,128]{2,1,0:T(8,128)} %get-tuple-element.15.small_ref), custom_call_target="tpu_custom_call" | custom-call | tf_op jit(solution)/shard_map/finish/pallas_call | solution.py:773

commit v4 on v3

--- a/solution.py
+++ b/solution.py
@@ -175,13 +175,6 @@
     pg_s,
     smsg,
     sgot,
-    pm_s,
-    actp_s,
-    mbuf,
-    mgot,
-    mtot,
-    qs,
-    qgot,
     gl,
     rb1,
     sb2,
@@ -204,8 +197,6 @@
     s_up,
     s_act,
     s_dh,
-    s_m,
-    s_qx,
     s_pair,
     s_col,
     s_third,
@@ -287,35 +278,45 @@
 
         loop(8, rows)
 
-    def part_to(msg, got, sems):
+    class Group:
+        def __init__(self, copy, sent, got, sems, at=0):
+            self.copy = copy
+            near = {"sp": lax.rem(me + 1, n)}
+            self.whole = remote(sent, got, sems, at, **near)
+
+    def part_to(msg, got, sems, at=0):
         def copy(k):
             j = lax.rem(me + k, n)
-            return remote(msg.at[j], got.at[k], sems, k, sp=j)
-
-        return copy
-
-    def part_from(mine, total, sems):
-        return lambda k: remote(mine, total.at[me], sems, k, sp=lax.rem(me + k, n))
-
-    def start_all(*copies):
+            return remote(msg.at[j], got.at[k], sems, at, sp=j)
+
+        rest = pl.ds(1, n - 1)
+        return Group(copy, msg.at[rest], got.at[rest], sems, at)
+
+    def part_from(mine, total, sems, at=0):
+        def copy(k):
+            return remote(mine, total.at[me], sems, at, sp=lax.rem(me + k, n))
+
+        rest = pl.ds(0, n - 1)
+        return Group(copy, total.at[rest], total.at[rest], sems, at)
+
+    def start_all(*groups):
         def start(k):
-            for copy in copies:
-                copy(k).start()
+            for group in groups:
+                group.copy(k).start()
 
         loop(n, start, 1)
 
-    def add_all(copy, got, own):
-        def add(k, total):
-            copy(k).wait_recv()
-            return total + got[k].astype(F32)
-
-        return lax.fori_loop(1, n, add, own)
-
-    def received(copy):
-        loop(n, lambda k: copy(k).wait_recv(), 1)
-
-    def sent(copy):
-        loop(n, lambda k: copy(k).wait_send(), 1)
+    def add_all(group, got, own):
+        received(group)
+        for k in range(1, n):
+            own = own + got[k].astype(F32)
+        return own
+
+    def received(group):
+        group.whole.wait_recv()
+
+    def sent(group):
+        group.whole.wait_send()
 
     def norm_one(i):
         at = ds(i * 32, 32)
@@ -353,31 +354,6 @@
     start_all(gram_out, sq_out)
     up_row = [up_ref.at[pl.ds(0, WIDTH)], up_ref.at[pl.ds(WIDTH, WIDTH)]]
 
-    def product_copy(p):
-        def copy(k):
-            j = lax.rem(me + k, n)
-            return remote(mbuf.at[p, j], mgot.at[p, k], s_m, n * p + k, sp=j)
-
-        return copy
-
-    def product(p):
-        for at in range(2):
-            cols = slice(512 * at + 128 * p, 512 * at + 128 * p + 128)
-            part = dot(actp_s[...], mixed_s[:, cols], 0, 0).astype(BF16)
-            mbuf[p, :, :, 128 * at : 128 * at + 128] = part.reshape(n, 16, 128)
-
-    lane = lax.broadcasted_iota(jnp.int32, (64, D), 1)
-    line = lax.broadcasted_iota(jnp.int32, (64, D), 0)
-    spot = (line >> 1) * 16 + (line & 1)
-    for r in range(8):
-        pm_s[64 * r : 64 * r + 64, :] = jnp.where(lane == spot + 2 * r, 1.0, 0.0).astype(BF16)
-    for i in range(0, TOK, 256):
-        actp_s[i : i + 256, :] = dot(act1_s[i : i + 256, :], pm_s[...], 1, 0).astype(BF16)
-    product(0)
-    start_all(product_copy(0))
-    for p in range(1, PAIRS):
-        product(p)
-
     for at in range(18):
         kern_ref[at : at + 1, :] = kern4_ref[(at // 3) % 3, at % 3, at // 9 : at // 9 + 1, :]
     for ref, count in ((act_s, 4), (up_s, 4), (dh_s, 4), (hid_s, 2)):
@@ -401,8 +377,6 @@
     start_all(gram_back, sq_back)
     send_above(up_row[0], up_halo, s_up)
     send_below(up_row[1], up_halo, s_up)
-    start_all(product_copy(1))
-    start_all(product_copy(3))
     loads[2].wait()
     received(gram_back)
     received(sq_back)
@@ -483,7 +457,6 @@
             send_above(dh_edge.at[0], dh_halo, s_dh)
         else:
             send_below(dh_edge.at[1], dh_halo, s_dh)
-    start_all(product_copy(2))
 
     def kernel_grads(idx):
         r = idx // 16
@@ -554,66 +527,79 @@
     small_out = part_to(smsg, sgot, s_s1)
     start_all(small_out)
 
-    def grads(block, left, right):
+    def grads(half, block, left, right):
         for side in range(2):
             g = dot(left[:, 256 * side : 256 * side + 256], right, 0, 0).astype(BF16)
             for r in range(4):
                 at = 4 * side + r
-                gl[at % 2, at // 2, :, 512 * block : 512 * block + 512] = g[64 * r : 64 * r + 64]
-
-    def pair_copy(k):
+                gl[half, at % 2, at // 2, :, 512 * block : 512 * block + 512] = g[
+                    64 * r : 64 * r + 64
+                ]
+
+    def pair_copy(half, k):
         there = lax.rem(y + 1 + k, 4)
-        return remote(gl.at[1 - core, there], rb1.at[k], s_pair, k, rep=2 * y + 1 - core)
-
-    def column_copy(k):
+        return remote(
+            gl.at[half, 1 - core, there],
+            rb1.at[half, k],
+            s_pair,
+            4 * half + k,
+            rep=2 * y + 1 - core,
+        )
+
+    def column_copy(half, k):
         there = lax.rem(y + 1 + k, 4)
-        return remote(sb2.at[k], rb2.at[k], s_col, k, rep=2 * there + core)
-
-    def pair_finish():
+        return remote(
+            sb2.at[half, k], rb2.at[half, k], s_col, 3 * half + k, rep=2 * there + core
+        )
+
+    def pair_start(half):
+        for k in range(4):
+            pair_copy(half, k).start()
+
+    def pair_finish(half):
         for k in range(3):
             there = lax.rem(y + 1 + k, 4)
-            pair_copy(k).wait_recv()
+            pair_copy(half, k).wait_recv()
 
             def add(i, k=k, there=there):
                 at = ds(i * 16, 16)
-                sb2[k, at, :] = (
-                    gl[core, there, at, :].astype(F32) + rb1[k, at, :].astype(F32)
+                sb2[half, k, at, :] = (
+                    gl[half, core, there, at, :].astype(F32) + rb1[half, k, at, :].astype(F32)
                 ).astype(BF16)
 
             loop(4, add)
-            column_copy(k).start()
-        pair_copy(3).wait_recv()
+            column_copy(half, k).start()
+        pair_copy(half, 3).wait_recv()
 
         def own(i):
             at = ds(i * 16, 16)
-            acc2[at, :] = gl[core, y, at, :].astype(F32) + rb1[3, at, :].astype(F32)
+            acc2[half, at, :] = gl[half, core, y, at, :].astype(F32) + rb1[half, 3, at, :].astype(
+                F32
+            )
 
         loop(4, own)
 
-    def third(k):
-        j = lax.rem(me + k, n)
-        return remote(sb3.at[j], rb3.at[k], s_third, k, sp=j)
-
-    def fourth(half):
-        return lambda k: remote(
-            fin.at[half], grads_ref.at[half, me], s_fourth, n * half + k, sp=lax.rem(me + k, n)
-        )
-
-    def column_finish():
+    third = [part_to(sb3.at[half], rb3.at[half], s_third, half) for half in range(2)]
+    fourth = [
+        part_from(fin.at[half], grads_ref.at[half], s_fourth, half) for half in range(2)
+    ]
+
+    def column_finish(half):
         for k in range(3):
-            column_copy(k).wait_recv()
+            column_copy(half, k).wait_recv()
         for j in range(n):
             rows, cols = chunk(j)
-            total = acc2[rows, cols]
+            total = acc2[half, rows, cols]
             for k in range(3):
-                total = total + rb2[k, rows, cols].astype(F32)
-            sb3[j] = total.astype(BF16)
-        start_all(third)
-
-    def to_everyone(half, total):
-        fin[half] = total.astype(BF16)
-        grads_ref[half, me] = total.astype(BF16)
-        start_all(fourth(half))
+                total = total + rb2[half, k, rows, cols].astype(F32)
+            sb3[half, j] = total.astype(BF16)
+        start_all(third[half])
+
+    def third_finish(half):
+        total = add_all(third[half], rb3.at[half], sb3[half, me].astype(F32)).astype(BF16)
+        fin[half] = total
+        grads_ref[half, me] = total
+        start_all(fourth[half])
 
     for p in range(PAIRS):
         cols = slice(128 * p, 128 * p + 128)
@@ -621,15 +607,10 @@
             dmix_s[i : i + 256, 2 * D + 128 * p : 2 * D + 128 * p + 128] = dot(
                 datt_s[i : i + 256, cols], bd_s[p], 1, 0
             ).astype(BF16)
-    grads(0, act1_s, dmix_s[:, 2 * D :])
-    grads(1, att_s, dproj_s[...])
-    for k in range(4):
-        pair_copy(k).start()
-    for p in range(PAIRS):
-        total = add_all(product_copy(p), mgot.at[p], mbuf[p, me].astype(F32))
-        mtot[:, 128 * p : 128 * p + 128] = total[:, :128]
-        mtot[:, D + 128 * p : D + 128 * p + 128] = total[:, 128:]
-    pair_finish()
+    grads(1, 0, act1_s, dmix_s[:, 2 * D :])
+    grads(1, 1, att_s, dproj_s[...])
+    pair_start(1)
+    pair_finish(1)
     total = add_all(prob_out, pgot, pmsg[me])
     pmine[...] = total
     start_all(prob_back)
@@ -639,19 +620,15 @@
     srb[rep] = total
 
     def small_copy(k):
-        return remote(ssend, srb.at[rep], s_small, k, rep=lax.rem(rep + k, reps))
+        return remote(ssend, srb.at[rep], s_small, 0, rep=lax.rem(rep + k, reps))
+
+    smalls = srb.at[pl.ds(0, reps - 1)]
+    small_all = remote(smalls, smalls, s_small, 0, rep=lax.rem(rep + 1, reps))
 
     for k in range(1, reps):
         small_copy(k).start()
-    column_finish()
     received(prob_back)
 
-    def split_dot(a, b, ca, cb):
-        high = a.astype(BF16)
-        rest = (a - high.astype(F32)).astype(BF16)
-        return dot(high, b, ca, cb) + dot(rest, b, ca, cb)
-
-    squares = []
     for p in range(PAIRS):
         prob, scores, divisor, sharp, query_norm, key_norm = pair_attention(
             p, gram_s, sq_s, sharp_ref, low, eye
@@ -663,24 +640,6 @@
         d_qsq = -half_sum(weighted, low) / (2.0 * query_norm * query_norm)
         d_qsq = 2.0 * jnp.sum(jnp.where(eye, d_qsq, 0.0), 0, keepdims=True)
         d_ksq = -2.0 * jnp.sum(weighted, 0, keepdims=True) / (2.0 * key_norm * key_norm)
-        squares.append((d_qsq, d_ksq))
-        by_query = mtot[:, 128 * p : 128 * p + 128]
-        by_key = mtot[:, D + 128 * p : D + 128 * p + 128]
-        g_query = split_dot(by_key, bd2_s[p], 1, 1) + d_qsq * by_query
-        g_key = split_dot(by_query, bd2_s[p], 1, 0) + d_ksq * by_key
-        for r in range(reps):
-            qs[r, 2 * p : 2 * p + 2, :] = g_query[2 * r : 2 * r + 2]
-            qs[r, 8 + 2 * p : 10 + 2 * p, :] = g_key[2 * r : 2 * r + 2]
-
-    def query_copy(k):
-        there = lax.rem(rep + k, reps)
-        return remote(qs.at[there], qgot.at[rep], s_qx, k, rep=there)
-
-    for k in range(1, reps):
-        query_copy(k).start()
-    qgot[rep] = qs[rep]
-    for p in range(PAIRS):
-        d_qsq, d_ksq = squares[p]
         qc = slice(128 * p, 128 * p + 128)
         kc = slice(D + 128 * p, D + 128 * p + 128)
         for i in range(0, TOK, 256):
@@ -693,15 +652,23 @@
         at = ds(i * 256, 256)
         dact_s[at, :] = dot(dmix_s[at, :], w_ref[...], 1, 1)
 
+    grads(0, 0, act1_s, dmix_s[:, :D])
+    grads(0, 1, act1_s, dmix_s[:, D : 2 * D])
+    pair_start(0)
+    column_finish(1)
+    pair_finish(0)
     loop(2, inputs)
-    for k in range(1, reps):
-        query_copy(k).wait_recv()
-    total = qgot[0]
-    for k in range(1, reps):
-        total = total + qgot[k]
-    to_everyone(0, total)
-    for k in range(1, reps):
-        small_copy(k).wait_recv()
+
+    def input_rows(i):
+        at = ds(i * 32, 32)
+        normed, inverse = norm_parts(x_ref[at, :].astype(F32))
+        lnb = norm_back(dact_s[at, :], gain1, normed, inverse)
+        out_ref[at, :] = (dres_s[at, :] + lnb).astype(BF16)
+
+    loop(TOK // 32, input_rows, each=4)
+    column_finish(0)
+    third_finish(1)
+    small_all.wait_recv()
     total = srb[0]
     for k in range(1, reps):
         total = total + srb[k]
@@ -709,34 +676,23 @@
     small_ref[me] = total
     fifth = part_from(sfin, small_ref, s_fifth)
     start_all(fifth)
-    to_everyone(1, add_all(third, rb3, sb3[me].astype(F32)))
-
-    def input_rows(i):
-        at = ds(i * 32, 32)
-        normed, inverse = norm_parts(x_ref[at, :].astype(F32))
-        lnb = norm_back(dact_s[at, :], gain1, normed, inverse)
-        out_ref[at, :] = (dres_s[at, :] + lnb).astype(BF16)
-
-    loop(TOK // 32, input_rows, each=4)
-
-    for copy in (gram_out, gram_back, sq_out, sq_back, prob_out, prob_back, small_out, third):
+    third_finish(0)
+
+    for copy in (gram_out, gram_back, sq_out, sq_back, prob_out, prob_back, small_out, third[0], third[1]):
         sent(copy)
-    for p in range(PAIRS):
-        sent(product_copy(p))
     for src, halo, sems in (
         (up_row[0], up_halo, s_up),
         (act_edge.at[0], act_halo, s_act),
         (dh_edge.at[0], dh_halo, s_dh),
     ):
         halos_sent(src, halo, sems)
-    for k in range(1, reps):
-        small_copy(k).wait_send()
-        query_copy(k).wait_send()
-    for k in range(4):
-        pair_copy(k).wait_send()
-    for k in range(3):
-        column_copy(k).wait_send()
-    for copy in (fourth(0), fifth, fourth(1)):
+    small_all.wait_send()
+    for half in range(2):
+        for k in range(4):
+            pair_copy(half, k).wait_send()
+        for k in range(3):
+            column_copy(half, k).wait_send()
+    for copy in (fourth[1], fifth, fourth[0]):
         received(copy)
         sent(copy)
 
@@ -745,9 +701,7 @@
     out_ref[...] = out_in[...]
     for j in range(32):
         rows, cols = chunk(j)
-        own = grads_ref[0, j].astype(F32)
-        for q in range(8):
-            gq_ref[2 * j : 2 * j + 2, 128 * q : 128 * q + 128] = own[2 * q : 2 * q + 2]
+        gq_ref[rows, cols] = grads_ref[0, j].astype(F32)
         if cols.start < D:
             gq_ref[rows, 2 * D + cols.start : 2 * D + cols.stop] = grads_ref[1, j].astype(F32)
         else:
@@ -799,22 +753,20 @@
     scratch += [wide, tall, tall, VMEM((TOK, 128), F32), tall, VMEM((18, 8, D), F32)]
     scratch += [wide, tall, wide, VMEM((TOK, 3 * D), BF16)]
     scratch += [row, row, VMEM((8, 128), F32), row, row, row]
-    scratch += [wide, wide, VMEM((PAIRS, n, 16, 256), BF16), VMEM((PAIRS, n, 16, 256), BF16)]
-    scratch += [VMEM((16, 1024), F32), VMEM((8, 16, 128), F32), VMEM((8, 16, 128), F32)]
     scratch += [
+        VMEM((2, 2, 4, 64, 1024), BF16),
         VMEM((2, 4, 64, 1024), BF16),
-        VMEM((4, 64, 1024), BF16),
-        VMEM((3, 64, 1024), BF16),
-        VMEM((3, 64, 1024), BF16),
-        VMEM((64, 1024), F32),
-        VMEM((n, 16, 128), BF16),
-        VMEM((n, 16, 128), BF16),
+        VMEM((2, 3, 64, 1024), BF16),
+        VMEM((2, 3, 64, 1024), BF16),
+        VMEM((2, 64, 1024), F32),
+        VMEM((2, n, 16, 128), BF16),
+        VMEM((2, n, 16, 128), BF16),
         VMEM((2, 16, 128), BF16),
         VMEM((8, 8, 128), F32),
         VMEM((8, 128), F32),
         VMEM((8, 128), F32),
     ]
-    for count in (3, n, n, n, n, n, n, n, 2, 2, 2, PAIRS * n, 8, 4, 3, n, 2 * n, 8, n):
+    for count in (3, 1, 1, 1, 1, 1, 1, 1, 2, 2, 2, 8, 6, 2, 2, 1, 1):
         scratch.append(pltpu.SemaphoreType.DMA((2, count)))
     out, grads, small = call(
         functools.partial(layer, n),

time: 112 us -> 95.1 us (0.85)
  Pallas kernels: 111 us -> 94.3 us
    pallas_call x2, Pallas kernels: 111 us -> 94.3 us  [call(): pl.pallas_call(body, name=name, out_shape=[jax.ShapeDtypeStruct(s, t) for...]
where the time goes in v4:
time: 95.1 us; the launch traced here: 94.9 us
  Pallas kernels  94.3 us (99%)
    pallas_call x2, Pallas kernels, call(): pl.pallas_call(body, name=name, out_shape=[jax.ShapeDtypeStruct(s, t) for...  94.3 us

profile of v4, /device:TPU:1, one launch (start us, length us, event | category | flops | bytes accessed | tf_op | source)
XLA Modules:
  0.0 94.9 jit_solution(12506561961012494880)
XLA Ops:
  0.6 92.1 %layer.1 = (bf16[512,512]{1,0:T(8,128)(2,1)}, bf16[2,32,16,128]{3,2,1,0:T(8,128)(2,1)}, f32[32,8,128]{2,1,0:T(8,128)}) custom-call(f32[8]{0:T(128)} %sharp_ref.1, bf16[512,512]{1,0:T(8,128)(2,1)} %bitcast.7, bf16[512,512]{1,0:T(8,128)(2,1)} %bitcast.8, f32[1,512]{1,0:T(1,128)} %bitcast.10, bf16[512,1536]{1,0:T(8,128)(2,1)} %w_hbm.1, ...), custom_call_target="tpu_custom_call" | custom-call | tf_op jit(solution)/shard_map/layer/pallas_call | solution.py:727
  92.8 2.2 %finish.1 = (bf16[512,512]{1,0:T(8,128)(2,1)}, f32[64,1536]{1,0:T(8,128)}, f32[64,512]{1,0:T(8,128)}, f32[3,3,2,512]{3,2,1,0:T(2,128)}, f32[2,512]{1,0:T(2,128)}) custom-call(bf16[512,512]{1,0:T(8,128)(2,1)} %get-tuple-element.13.out_in, bf16[2,32,16,128]{3,2,1,0:T(8,128)(2,1)} %get-tuple-element.14.grads_ref, f32[32,8,128]{2,1,0:T(8,128)} %get-tuple-element.15.small_ref), custom_call_target="tpu_custom_call" | custom-call | tf_op jit(solution)/shard_map/finish/pallas_call | solution.py:727

commit v5 on v4

--- a/solution.py
+++ b/solution.py
@@ -120,18 +120,24 @@
 
 def layer(
     n,
+    sharp_hbm,
+    x_hbm,
+    up_hbm,
+    gain1_hbm,
+    w_hbm,
+    wo_hbm,
+    factor_hbm,
+    gain2_hbm,
+    kern4_hbm,
+    out_ref,
+    grads_ref,
+    small_ref,
     sharp_ref,
     x_ref,
-    up_hbm,
     gain1_ref,
-    w_hbm,
-    wo_hbm,
     factor_ref,
     gain2_ref,
     kern4_ref,
-    out_ref,
-    grads_ref,
-    small_ref,
     up_ref,
     w_ref,
     wo_ref,
@@ -206,14 +212,24 @@
 ):
     me, rep = lax.axis_index("sp"), lax.axis_index("rep")
     reps = 8
+    moves = (
+        (x_hbm, x_ref),
+        (gain1_hbm, gain1_ref),
+        (w_hbm, w_ref),
+        (up_hbm, up_ref),
+        (wo_hbm, wo_ref),
+        (sharp_hbm, sharp_ref),
+        (factor_hbm, factor_ref),
+        (gain2_hbm, gain2_ref),
+        (kern4_hbm, kern4_ref),
+    )
     loads = [
-        pltpu.make_async_copy(src, dst, s_load.at[0, at])
-        for at, (src, dst) in enumerate(((w_hbm, w_ref), (up_hbm, up_ref), (wo_hbm, wo_ref)))
+        pltpu.make_async_copy(src, dst, s_load.at[0, at]) for at, (src, dst) in enumerate(moves)
     ]
-    for load in loads:
-        load.start()
     y, core = rep // 2, lax.rem(rep, 2)
     barrier = pltpu.get_barrier_semaphore()
+    loads[0].start()
+    loads[1].start()
 
     def greet(k):
         pl.semaphore_signal(
@@ -225,9 +241,9 @@
         pl.semaphore_signal(
             barrier, inc=1, device_id={"rep": lax.rem(rep + k, reps)}, device_id_type=MESH_ID
         )
+    for load in loads[2:]:
+        load.start()
     low, eye = lane_low(), eye_pair()
-    gain1, gain2 = gain1_ref[...], gain2_ref[...]
-    factor0, factor1 = factor_ref[0:1, :], factor_ref[1:2, :]
 
     def to_above(src, halo, sems):
         return remote(src, halo.at[1], sems, 0, sp=me - 1)
@@ -300,7 +316,8 @@
         return Group(copy, total.at[rest], total.at[rest], sems, at)
 
     def start_all(*groups):
-        def start(k):
+        def start(t):
+            k = n // 2 + (t // 2) * (1 - 2 * lax.rem(t, 2))
             for group in groups:
                 group.copy(k).start()
 
@@ -318,13 +335,17 @@
     def sent(group):
         group.whole.wait_send()
 
+    loads[0].wait()
+    loads[1].wait()
+    gain1 = gain1_ref[...]
+
     def norm_one(i):
         at = ds(i * 32, 32)
         normed, _ = norm_parts(x_ref[at, :].astype(F32))
         act1_s[at, :] = (normed * gain1).astype(BF16)
 
     loop(TOK // 32, norm_one, each=4)
-    loads[0].wait()
+    loads[2].wait()
 
     def mix(i):
         at = ds(i * 256, 256)
@@ -354,6 +375,10 @@
     start_all(gram_out, sq_out)
     up_row = [up_ref.at[pl.ds(0, WIDTH)], up_ref.at[pl.ds(WIDTH, WIDTH)]]
 
+    for load in loads[3:]:
+        load.wait()
+    gain2 = gain2_ref[...]
+    factor0, factor1 = factor_ref[0:1, :], factor_ref[1:2, :]
     for at in range(18):
         kern_ref[at : at + 1, :] = kern4_ref[(at // 3) % 3, at % 3, at // 9 : at // 9 + 1, :]
     for ref, count in ((act_s, 4), (up_s, 4), (dh_s, 4), (hid_s, 2)):
@@ -366,7 +391,6 @@
         row, c = i // 4, lax.rem(i, 4)
         up_s[row + 1, ds(8 + c * 64, 64, 8), :] = up_ref[ds(i * 64, 64), :].astype(F32)
 
-    loads[1].wait()
     loop(8, upstream_rows)
     total = add_all(gram_out, ggot, gmsg[me])
     gmine[...] = total
@@ -377,7 +401,6 @@
     start_all(gram_back, sq_back)
     send_above(up_row[0], up_halo, s_up)
     send_below(up_row[1], up_halo, s_up)
-    loads[2].wait()
     received(gram_back)
     received(sq_back)
     for p in range(2 * PAIRS):
@@ -436,6 +459,25 @@
         dhid_s[ds(r * WIDTH + c * 64, 64), lanes] = back(sums)
 
     loop(32, hidden_grads)
+
+    def own_part(target, source, rows, join):
+        for r in range(2):
+
+            def go(idx, r=r):
+                lanes, c = place(idx)
+                win = ds(c * 64, 80, 8)
+                near = {i: source[rows(r, i), win, lanes] for i in range(3) if rows(r, i) in (1, 2)}
+                target[ds(r * WIDTH + c * 64, 64), lanes] = join(
+                    [sum(taps(0, lanes, i, j) * near[i] for i in near) for j in range(3)]
+                )
+
+            loop(16, go)
+
+    def halo_part(source, row, i, win, lanes, join):
+        near = source[row, win, lanes]
+        return join([taps(0, lanes, i, j) * near for j in range(3)])
+
+    own_part(dact_s, act_s, lambda r, i: r + i, forth)
     halos_in(act_edge.at[0], act_halo, s_act)
     spread(act_halo, act_s)
     for r in range(2):
@@ -443,8 +485,9 @@
         def hidden_row(idx, r=r):
             lanes, c = place(idx)
             win, mid = ds(c * 64, 80, 8), ds(8 + c * 64, 64, 8)
-            near = [act_s[r + i, win, lanes] for i in range(3)]
-            h = forth([sum(taps(0, lanes, i, j) * near[i] for i in range(3)) for j in range(3)])
+            h = dact_s[ds(r * WIDTH + c * 64, 64), lanes] + halo_part(
+                act_s, 3 * r, 2 * r, win, lanes, forth
+            )
             cumul = 0.5 * (1.0 + lax.erf(h * 0.7071067811865476))
             density = jnp.exp(-0.5 * h * h) * 0.3989422804014327
             hid_s[r, mid, lanes] = (h * cumul).astype(BF16).astype(F32)
@@ -476,18 +519,20 @@
                 acc_s[9 + 3 * i + j, :, lanes] += fold(moved[j] * up)
 
     loop(32, kernel_grads)
+    own_part(dact_s, dh_s, lambda r, i: r + 2 - i, back)
     halos_in(dh_edge.at[0], dh_halo, s_dh)
     spread(dh_halo, dh_s)
 
-    def act_grads(idx):
-        r = idx // 16
-        lanes, c = place(lax.rem(idx, 16))
-        win = ds(c * 64, 80, 8)
-        near = [dh_s[r + 2 - i, win, lanes] for i in range(3)]
-        sums = [sum(taps(0, lanes, i, j) * near[i] for i in range(3)) for j in range(3)]
-        dact_s[ds(r * WIDTH + c * 64, 64), lanes] = back(sums)
-
-    loop(32, act_grads)
+    for r in range(2):
+
+        def act_grads(idx, r=r):
+            lanes, c = place(idx)
+            win, at = ds(c * 64, 80, 8), ds(r * WIDTH + c * 64, 64)
+            dact_s[at, lanes] = dact_s[at, lanes] + halo_part(
+                dh_s, 3 * r, 2 - 2 * r, win, lanes, back
+            )
+
+        loop(16, act_grads)
 
     def residual_rows(step, scale):
         for u in range(4):
@@ -743,7 +788,9 @@
     row = VMEM((n, 8, 128), F32)
     edge = VMEM((2, WIDTH, D), BF16)
     wide, tall = VMEM((TOK, D), BF16), VMEM((TOK, D), F32)
-    scratch = [wide, VMEM((D, 3 * D), BF16), wide, wide, VMEM((TOK, 3 * D), BF16)]
+    scratch = [pltpu.SMEM((HEADS,), F32), wide, VMEM((1, D), F32), VMEM((2, D), F32)]
+    scratch += [VMEM((1, D), F32), VMEM((3, 3, 2, D), F32)]
+    scratch += [wide, VMEM((D, 3 * D), BF16), wide, wide, VMEM((TOK, 3 * D), BF16)]
     scratch += [row, row, VMEM((8, 128), F32), row]
     scratch += [VMEM((n, 1, 128), F32), VMEM((n, 1, 128), F32), VMEM((1, 128), F32)]
     scratch += [VMEM((n, 1, 128), F32), VMEM((8, 128), F32), VMEM((18, D), F32)]
@@ -766,7 +813,7 @@
         VMEM((8, 128), F32),
         VMEM((8, 128), F32),
     ]
-    for count in (3, 1, 1, 1, 1, 1, 1, 1, 2, 2, 2, 8, 6, 2, 2, 1, 1):
+    for count in (9, 1, 1, 1, 1, 1, 1, 1, 2, 2, 2, 8, 6, 2, 2, 1, 1):
         scratch.append(pltpu.SemaphoreType.DMA((2, count)))
     out, grads, small = call(
         functools.partial(layer, n),
@@ -774,9 +821,8 @@
         [((TOK, D), BF16), ((2, n, 16, 128), BF16), ((n, 8, 128), F32)],
         scratch,
         (sharp, x, up, gain1, w, wo, factors, gain2, kernels),
-        smem=1,
         collective=0,
-        away=(2, 4, 5),
+        away=range(9),
     )
     out, gq, gp, conv, scale = call(
         finish,

time: 95.1 us -> 89.3 us (0.939)
  Pallas kernels: 94.3 us -> 88.5 us
    pallas_call x2, Pallas kernels: 94.3 us -> 88.5 us  [call(): pl.pallas_call(body, name=name, out_shape=[jax.ShapeDtypeStruct(s, t) for...]
where the time goes in v5:
time: 89.3 us; the launch traced here: 89.1 us
  Pallas kernels  88.5 us (99%)
    pallas_call x2, Pallas kernels, call(): pl.pallas_call(body, name=name, out_shape=[jax.ShapeDtypeStruct(s, t) for...  88.5 us

profile of v5, /device:TPU:1, one launch (start us, length us, event | category | flops | bytes accessed | tf_op | source)
XLA Modules:
  0.0 89.1 jit_solution(17703131554242406173)
XLA Ops:
  0.6 86.3 %layer.1 = (bf16[512,512]{1,0:T(8,128)(2,1)}, bf16[2,32,16,128]{3,2,1,0:T(8,128)(2,1)}, f32[32,8,128]{2,1,0:T(8,128)}) custom-call(f32[8]{0:T(128)} %sharp_hbm.1, bf16[512,512]{1,0:T(8,128)(2,1)} %bitcast.7, bf16[512,512]{1,0:T(8,128)(2,1)} %bitcast.8, f32[1,512]{1,0:T(1,128)} %bitcast.10, bf16[512,1536]{1,0:T(8,128)(2,1)} %w_hbm.1, ...), custom_call_target="tpu_custom_call" | custom-call | tf_op jit(solution)/shard_map/layer/pallas_call | solution.py:772
  87.0 2.2 %finish.1 = (bf16[512,512]{1,0:T(8,128)(2,1)}, f32[64,1536]{1,0:T(8,128)}, f32[64,512]{1,0:T(8,128)}, f32[3,3,2,512]{3,2,1,0:T(2,128)}, f32[2,512]{1,0:T(2,128)}) custom-call(bf16[512,512]{1,0:T(8,128)(2,1)} %get-tuple-element.13.out_in, bf16[2,32,16,128]{3,2,1,0:T(8,128)(2,1)} %get-tuple-element.14.grads_ref, f32[32,8,128]{2,1,0:T(8,128)} %get-tuple-element.15.small_ref), custom_call_target="tpu_custom_call" | custom-call | tf_op jit(solution)/shard_map/finish/pallas_call | solution.py:772

commit v6 on v5

--- a/solution.py
+++ b/solution.py
@@ -245,26 +245,33 @@
         load.start()
     low, eye = lane_low(), eye_pair()
 
-    def to_above(src, halo, sems):
-        return remote(src, halo.at[1], sems, 0, sp=me - 1)
-
-    def to_below(src, halo, sems):
-        return remote(src, halo.at[0], sems, 1, sp=me + 1)
-
-    def send_above(src, halo, sems):
+    half_row = WIDTH // 2
+
+    def to_above(src, halo, sems, half):
+        at = pl.ds(half * half_row, half_row)
+        return remote(src.at[at], halo.at[1, at], sems, half, sp=me - 1)
+
+    def to_below(src, halo, sems, half):
+        at = pl.ds(half * half_row, half_row)
+        return remote(src.at[at], halo.at[0, at], sems, 2 + half, sp=me + 1)
+
+    def send_above(src, halo, sems, halves=(0, 1)):
         @pl.when(me > 0)
         def _():
-            to_above(src, halo, sems).start()
-
-    def send_below(src, halo, sems):
+            for half in halves:
+                to_above(src, halo, sems, half).start()
+
+    def send_below(src, halo, sems, halves=(0, 1)):
         @pl.when(me < n - 1)
         def _():
-            to_below(src, halo, sems).start()
+            for half in halves:
+                to_below(src, halo, sems, half).start()
 
     def halos_in(src, halo, sems):
         @pl.when(me > 0)
         def _():
-            to_below(src, halo, sems).wait_recv()
+            for half in range(2):
+                to_below(src, halo, sems, half).wait_recv()
 
         @pl.when(me == 0)
         def _():
@@ -272,7 +279,8 @@
 
         @pl.when(me < n - 1)
         def _():
-            to_above(src, halo, sems).wait_recv()
+            for half in range(2):
+                to_above(src, halo, sems, half).wait_recv()
 
         @pl.when(me == n - 1)
         def _():
@@ -281,11 +289,13 @@
     def halos_sent(src, halo, sems):
         @pl.when(me > 0)
         def _():
-            to_above(src, halo, sems).wait_send()
+            for half in range(2):
+                to_above(src, halo, sems, half).wait_send()
 
         @pl.when(me < n - 1)
         def _():
-            to_below(src, halo, sems).wait_send()
+            for half in range(2):
+                to_below(src, halo, sems, half).wait_send()
 
     def spread(halo, target):
         def rows(i):
@@ -417,7 +427,10 @@
             att_s[at_row, cols] = dot(value, bd_s[p], 1, 1).astype(BF16)
         proj_s[at_row, :] = dot(att_s[at_row, :], wo_ref[...], 1, 0)
 
-        def norm_two(c, row=row):
+    for half, row in ((0, 0), (0, 1), (1, 0), (1, 1)):
+
+        def norm_two(i, half=half, row=row):
+            c = 4 * half + i
             at = ds(row * WIDTH + c * 32, 32)
             u = x_ref[at, :].astype(F32) + factor0 * proj_s[at, :]
             normed, inverse = norm_parts(u.astype(BF16).astype(F32))
@@ -427,11 +440,11 @@
             normed_s[at, :] = normed
             inv_s[at, :] = jnp.broadcast_to(inverse, (32, 128))
 
-        loop(WIDTH // 32, norm_two, each=4)
+        loop(4, norm_two, each=4)
         if row == 0:
-            send_above(act_edge.at[0], act_halo, s_act)
+            send_above(act_edge.at[0], act_halo, s_act, (half,))
         else:
-            send_below(act_edge.at[1], act_halo, s_act)
+            send_below(act_edge.at[1], act_halo, s_act, (half,))
 
     def taps(which, lanes, i, j):
         at = 9 * which + 3 * i + j
@@ -480,10 +493,10 @@
     own_part(dact_s, act_s, lambda r, i: r + i, forth)
     halos_in(act_edge.at[0], act_halo, s_act)
     spread(act_halo, act_s)
-    for r in range(2):
-
-        def hidden_row(idx, r=r):
-            lanes, c = place(idx)
+    for half, r in ((0, 0), (0, 1), (1, 0), (1, 1)):
+
+        def hidden_row(idx, half=half, r=r):
+            lanes, c = ds((idx // 2) * 128, 128), 2 * half + lax.rem(idx, 2)
             win, mid = ds(c * 64, 80, 8), ds(8 + c * 64, 64, 8)
             h = dact_s[ds(r * WIDTH + c * 64, 64), lanes] + halo_part(
                 act_s, 3 * r, 2 * r, win, lanes, forth
@@ -495,11 +508,11 @@
             dh_s[r + 1, mid, lanes] = d_h
             dh_edge[r, ds(c * 64, 64), lanes] = d_h.astype(BF16)
 
-        loop(16, hidden_row)
+        loop(8, hidden_row)
         if r == 0:
-            send_above(dh_edge.at[0], dh_halo, s_dh)
+            send_above(dh_edge.at[0], dh_halo, s_dh, (half,))
         else:
-            send_below(dh_edge.at[1], dh_halo, s_dh)
+            send_below(dh_edge.at[1], dh_halo, s_dh, (half,))
 
     def kernel_grads(idx):
         r = idx // 16
@@ -813,7 +826,7 @@
         VMEM((8, 128), F32),
         VMEM((8, 128), F32),
     ]
-    for count in (9, 1, 1, 1, 1, 1, 1, 1, 2, 2, 2, 8, 6, 2, 2, 1, 1):
+    for count in (9, 1, 1, 1, 1, 1, 1, 1, 4, 4, 4, 8, 6, 2, 2, 1, 1):
         scratch.append(pltpu.SemaphoreType.DMA((2, count)))
     out, grads, small = call(
         functools.partial(layer, n),

time: 89.3 us -> 89.4 us (level)
  no operation moved by 1% of the time
where the time goes in v6:
time: 89.4 us; the launch traced here: 89.2 us
  Pallas kernels  88.6 us (99%)
    pallas_call x2, Pallas kernels, call(): pl.pallas_call(body, name=name, out_shape=[jax.ShapeDtypeStruct(s, t) for...  88.6 us

profile of v6, /device:TPU:1, one launch (start us, length us, event | category | flops | bytes accessed | tf_op | source)
XLA Modules:
  0.0 89.2 jit_solution(14795917528667353865)
XLA Ops:
  0.6 86.4 %layer.1 = (bf16[512,512]{1,0:T(8,128)(2,1)}, bf16[2,32,16,128]{3,2,1,0:T(8,128)(2,1)}, f32[32,8,128]{2,1,0:T(8,128)}) custom-call(f32[8]{0:T(128)} %sharp_hbm.1, bf16[512,512]{1,0:T(8,128)(2,1)} %bitcast.7, bf16[512,512]{1,0:T(8,128)(2,1)} %bitcast.8, f32[1,512]{1,0:T(1,128)} %bitcast.10, bf16[512,1536]{1,0:T(8,128)(2,1)} %w_hbm.1, ...), custom_call_target="tpu_custom_call" | custom-call | tf_op jit(solution)/shard_map/layer/pallas_call | solution.py:785
  87.1 2.2 %finish.1 = (bf16[512,512]{1,0:T(8,128)(2,1)}, f32[64,1536]{1,0:T(8,128)}, f32[64,512]{1,0:T(8,128)}, f32[3,3,2,512]{3,2,1,0:T(2,128)}, f32[2,512]{1,0:T(2,128)}) custom-call(bf16[512,512]{1,0:T(8,128)(2,1)} %get-tuple-element.13.out_in, bf16[2,32,16,128]{3,2,1,0:T(8,128)(2,1)} %get-tuple-element.14.grads_ref, f32[32,8,128]{2,1,0:T(8,128)} %get-tuple-element.15.small_ref), custom_call_target="tpu_custom_call" | custom-call | tf_op jit(solution)/shard_map/finish/pallas_call | solution.py:785
